TPU v7x, 16 devices: a whole 2x2x2 slice. The times are simulated.
16 devices in a mesh: ep: 16 (over z, y, x, core).
Axes of the slice: x: 2, y: 2, z: 2, core: 2. Of those that a mesh axis runs over, the one named last changes fastest.
Arguments:
- tokens: bfloat16 [256, 256, 768], P('ep')
- pad_mask: int32 [256, 256], P('ep')
- second_draw: float32 [256, 256], P('ep')
- choices: int32 [256, 256, 2], P('ep')
- norm_attn: float32 [768], replicated
- w_query: bfloat16 [768, 12, 64], replicated
- w_key: bfloat16 [768, 12, 64], replicated
- w_value: bfloat16 [768, 12, 64], replicated
- w_attn_out: bfloat16 [12, 64, 768], replicated
- norm_moe: float32 [768], replicated
- w_gate: float32 [768, 128], replicated
- w_in: bfloat16 [128, 768, 3072], P('ep')
- w_out: bfloat16 [128, 3072, 768], P('ep')
Outputs:
- output 1: bfloat16 [256, 256, 768], P('ep')
- output 2: float32 [], replicated
All inputs are finite; a program needn't handle non-finite values.
Results may differ from a plain program's by a relative error of at most 0.0175475.
Values are sent between devices in bfloat16 or wider.
A program may use at most 1 GiB of HBM per device.

v0:
```python
import functools
import jax
import jax.numpy as jnp
from jax import lax
from jax.experimental import pallas as pl
from jax.experimental.pallas import tpu as pltpu
from jax.sharding import PartitionSpec as P

NORM_EPS = 1e-6
N_DEV = 16
MESH = pl.DeviceIdType.MESH
F32 = jnp.float32
BF16 = jnp.bfloat16
ORDER = (0, 9, 2, 11, 4, 13, 6, 15, 8, 1, 10, 3, 12, 5, 14, 7)
VMEM_LIMIT = 62 * 1024 * 1024


def partner(me, mask):
    out = 0
    for bit in range(4):
        val = lax.rem(me // (1 << bit), 2)
        out = out + (1 << bit) * ((1 - val) if (mask >> bit) & 1 else val)
    return out


def greet(me):
    barrier = pltpu.get_barrier_semaphore()
    for mask in range(1, N_DEV):
        pl.semaphore_signal(barrier, inc=1, device_id=(partner(me, mask),), device_id_type=MESH)


def rms_norm(values_f, scale_vec):
    inv_rms = lax.rsqrt(jnp.mean(values_f * values_f, axis=-1, keepdims=True) + NORM_EPS)
    return (values_f * inv_rms * scale_vec).astype(BF16)


def dot(a, b):
    return jnp.dot(a, b, preferred_element_type=F32)


def dot_nt(a, b):
    return lax.dot_general(a, b, (((1,), (1,)), ((), ())), preferred_element_type=F32)


def split_gate(wgate_ref, wg_s):
    experts = wgate_ref.shape[1]
    wg = wgate_ref[...].T
    hi = wg.astype(BF16)
    rest = wg - hi.astype(F32)
    mid = rest.astype(BF16)
    low = (rest - mid.astype(F32)).astype(BF16)
    wg_s[0:experts] = hi
    wg_s[experts:2 * experts] = mid
    wg_s[2 * experts:3 * experts] = low


def attend(
    step, tokens_ref, pad_ref, norm_attn_ref, wq_ref, wk_ref, wv_ref, wo_ref, norm_moe_ref, hidden_ref,
    q_s, k_s, v_s, ctx_s, s_s, p_s, wg_s, heads, head_dim, experts,
):
    seq = tokens_ref.shape[1]
    d_model = tokens_ref.shape[2]
    x = tokens_ref[...].reshape(2 * seq, d_model)
    a = rms_norm(x.astype(F32), norm_attn_ref[...][None, :])
    q_s[...] = dot_nt(wq_ref[...], a).astype(BF16)
    k_s[...] = dot_nt(a, wk_ref[...]).astype(BF16)
    v_s[...] = dot_nt(wv_ref[...], a).astype(BF16)

    width = 2 * head_dim
    lane = lax.broadcasted_iota(jnp.int32, (1, width), 1)
    scale = head_dim ** -0.5
    sides = [jnp.where(lane < head_dim, scale, 0.0).astype(BF16), jnp.where(lane < head_dim, 0.0, scale).astype(BF16)]
    cut = seq // 2
    late_key = lax.broadcasted_iota(jnp.int32, (seq - cut, 128), 0) + cut
    batch = s_s.shape[1]
    lanes = 128
    buf = 0
    for grp in range(2):
        tok = pl.ds(grp * seq, seq)
        length = jnp.sum(pad_ref[pl.ds(2 * step + grp, 1), :], axis=1, keepdims=True)
        keep_late = late_key < length
        for first in range(0, heads, batch):
            for i in range(batch):
                off = (first + i) // 2 * width
                k = k_s[tok, pl.ds(off, width)] * sides[(first + i) % 2]
                s_s[buf, i] = dot(k, q_s[pl.ds(off, width), tok])
            for i in range(batch):
                for col in range(0, seq, lanes):
                    cols = pl.ds(col, lanes)
                    early = s_s[buf, i, pl.ds(0, cut), cols]
                    late = jnp.where(keep_late, s_s[buf, i, pl.ds(cut, seq - cut), cols], -1e30)
                    top = jnp.maximum(jnp.max(early, axis=0, keepdims=True), jnp.max(late, axis=0, keepdims=True))
                    early = jnp.exp(early - top)
                    late = jnp.exp(late - top)
                    inv = 1.0 / (jnp.sum(early, axis=0, keepdims=True) + jnp.sum(late, axis=0, keepdims=True))
                    p_s[buf, i, pl.ds(0, cut), cols] = (early * inv).astype(BF16)
                    p_s[buf, i, pl.ds(cut, seq - cut), cols] = (late * inv).astype(BF16)
            for i in range(batch):
                head = pl.ds((first + i) * head_dim, head_dim)
                ctx_s[head, tok] = dot(v_s[head, tok], p_s[buf, i]).astype(BF16)
            buf = 1 - buf

    attn = lax.dot_general(ctx_s[...], wo_ref[...], (((0,), (0,)), ((), ())), preferred_element_type=F32)
    hidden = (x.astype(F32) + attn).astype(BF16)
    hidden_ref[...] = hidden.reshape(2, seq, d_model)
    b = rms_norm(hidden.astype(F32), norm_moe_ref[...][None, :])
    lg = dot_nt(wg_s[...], b)
    logits = (lg[2 * experts:] + lg[experts:2 * experts]) + lg[:experts]
    ex = jnp.exp(logits - jnp.max(logits, axis=0, keepdims=True))
    return b, ex / jnp.sum(ex, axis=0, keepdims=True)


def full_front_kernel(hidden_ref, meta_ref, norm_moe_ref, recv_ref, send_s, send_sem, recv_sem, own_sem, *, experts, capacity):
    step = pl.program_id(0)
    steps = pl.num_programs(0)
    me = lax.axis_index("ep")
    seq = hidden_ref.shape[1]
    d_model = hidden_ref.shape[2]
    e_loc = experts // N_DEV
    half = e_loc // 2
    slots = experts * capacity
    rows = 2 * capacity
    per_src = steps * rows

    def send_pair(pair):
        for place, mask in enumerate(ORDER):
            dev = partner(me, mask)
            src = send_s.at[pair, dev]
            dst = recv_ref.at[:, pl.ds(pl.multiple_of(place * per_src + pair * rows, rows), rows), :]
            if mask == 0:
                pltpu.make_async_copy(src, dst, own_sem).start()
            else:
                pltpu.make_async_remote_copy(
                    src_ref=src, dst_ref=dst, send_sem=send_sem, recv_sem=recv_sem,
                    device_id=(dev,), device_id_type=MESH).start()

    @pl.when(step == 0)
    def _():
        greet(me)

    @pl.when(step == 1)
    def _():
        pl.semaphore_wait(pltpu.get_barrier_semaphore(), N_DEV - 1)

    @pl.when(step > 0)
    def _():
        send_pair(step - 1)

    slot_id = lax.broadcasted_iota(jnp.int32, (slots, seq), 0)
    picked = []
    for grp in range(2):
        b = rms_norm(hidden_ref[grp].astype(F32), norm_moe_ref[...][None, :])

        def place_of(code):
            e = code // capacity
            dev = e // e_loc
            r = e - dev * e_loc
            upper = r // half
            side = upper if grp == 0 else 1 - upper
            at = ((dev * half + r - upper * half) * 2 + side) * capacity + code - e * capacity
            return jnp.where(code >= 0, at, -1)

        d1 = place_of(meta_ref[grp, 4:5, :].astype(jnp.int32))
        d2 = place_of(meta_ref[grp, 5:6, :].astype(jnp.int32))
        disp_mat = jnp.where((slot_id == d1) | (slot_id == d2), 1.0, 0.0).astype(BF16)
        picked.append(dot(disp_mat, b).reshape(N_DEV * half, rows, d_model))

    top = lax.broadcasted_iota(jnp.int32, (1, rows, 1), 1) < capacity
    lower = jnp.where(top, picked[0], picked[1]).astype(BF16)
    upper = jnp.where(top, picked[1], picked[0]).astype(BF16)
    send_s[step, :, 0:half] = lower.reshape(N_DEV, half, rows, d_model)
    send_s[step, :, half:e_loc] = upper.reshape(N_DEV, half, rows, d_model)

    @pl.when(step == steps - 1)
    def _():
        send_pair(steps - 1)
        others = pl.ds(0, N_DEV - 1)
        pltpu.make_async_copy(send_s.at[:, others], send_s.at[:, others], send_sem).wait()
        pltpu.make_async_copy(send_s.at[:, 0], send_s.at[:, 0], own_sem).wait()
        arrived = recv_ref.at[:, pl.ds(0, (N_DEV - 1) * per_src), :]
        pltpu.make_async_copy(arrived, arrived, recv_sem).wait()


def expert_kernel(recv_ref, w_in_ref, w_out_ref, ret_ref, act_s, z_s, send_sem, recv_sem, local_sem, *, tile):
    e = pl.program_id(0)
    n_exp = pl.num_programs(0)
    me = lax.axis_index("ep")
    rows = recv_ref.shape[1]
    ff = w_in_ref.shape[2]
    per_src = rows // N_DEV
    n_tiles = rows // tile
    chunk = 1024

    @pl.when(e == 0)
    def _():
        greet(me)

    def run(t, carry):
        at = pl.ds(pl.multiple_of(t * tile, tile), tile)
        x = recv_ref[0, at, :]
        for f in range(ff // chunk):
            act = dot(x, w_in_ref[0, :, pl.ds(f * chunk, chunk)])
            act_s[:, pl.ds(f * chunk, chunk)] = jnp.maximum(act, 0.0).astype(BF16)
        z_s[e, at, :] = dot(act_s[...], w_out_ref[0]).astype(BF16)
        return carry

    lax.fori_loop(0, n_tiles, run, 0)

    @pl.when(e == 0)
    def _():
        pl.semaphore_wait(pltpu.get_barrier_semaphore(), N_DEV - 1)

    for place, mask in enumerate(ORDER):
        dev = partner(me, mask)
        src = z_s.at[e, pl.ds(place * per_src, per_src), :]
        dst = ret_ref.at[me * n_exp + e]
        if mask == 0:
            pltpu.make_async_copy(src, dst, local_sem).start()
        else:
            pltpu.make_async_remote_copy(
                src_ref=src, dst_ref=dst, send_sem=send_sem, recv_sem=recv_sem,
                device_id=(dev,), device_id_type=MESH).start()

    @pl.when(e == n_exp - 1)
    def _():
        sent = z_s.at[:, pl.ds(0, (N_DEV - 1) * per_src), :]
        pltpu.make_async_copy(sent, sent, send_sem).wait()
        own = z_s.at[:, pl.ds(0, per_src), :]
        pltpu.make_async_copy(own, own, local_sem).wait()
        arrived = ret_ref.at[pl.ds(0, (N_DEV - 1) * n_exp)]
        pltpu.make_async_copy(arrived, arrived, recv_sem).wait()


def back_kernel(ret_ref, hidden_ref, meta_ref, msg_ref, out_ref, aux_ref, *, n_groups, capacity):
    experts, rows, d_model = ret_ref.shape
    seq = hidden_ref.shape[1]
    z = ret_ref[...].reshape(experts * rows, d_model)
    slot_id = lax.broadcasted_iota(jnp.int32, (seq, experts * rows), 1)
    e_loc = experts // N_DEV
    for grp in range(2):
        meta = meta_ref[grp].T

        def place_of(code):
            e = code // capacity
            r = e - e // e_loc * e_loc
            upper = r // (e_loc // 2)
            side = upper if grp == 0 else 1 - upper
            return jnp.where(code >= 0, (e * 2 + side) * capacity + code - e * capacity, -1)

        c1 = place_of(meta[:, 4:5].astype(jnp.int32))
        c2 = place_of(meta[:, 5:6].astype(jnp.int32))
        comb = jnp.where(slot_id == c1, meta[:, 2:3], 0.0) + jnp.where(slot_id == c2, meta[:, 3:4], 0.0)
        moe = dot(comb.astype(BF16), z)
        out_ref[grp] = (hidden_ref[grp].astype(F32) + moe).astype(BF16)

    @pl.when(pl.program_id(0) == 0)
    def _():
        total = jnp.sum(msg_ref[:, 0:8, :], axis=0)
        total = jnp.sum(jnp.sum(total, axis=1, keepdims=True), axis=0, keepdims=True)
        aux_ref[...] = jnp.broadcast_to(total * (experts / n_groups), aux_ref.shape)


FIX = 8
LOCAL = 48
PACK = 112
EXTRA = 32
TEAM = 4
POOL = 80


def twice(value):
    return jnp.concatenate([value, value], axis=1)


def packed_front_kernel(
    tokens_ref, pad_ref, draw_ref, choices_ref, norm_attn_ref, wq_ref, wk_ref, wv_ref, wo_ref, norm_moe_ref, wgate_ref,
    hidden_ref, meta_ref, fix_ref, pack_ref, msg_ref,
    q_s, k_s, v_s, ctx_s, s_s, p_s, wg_s, b_s, slot_s, count_s, aux_s, flag_s, code_s, goal_s,
    local_s, fix_s, pack_s, msg_s, fix_send, fix_recv, pack_send, pack_recv, msg_send, msg_recv, own_sem,
    *, heads, head_dim, capacity,
):
    step = pl.program_id(0)
    steps = pl.num_programs(0)
    quad = step // 2
    quads = steps // 2
    me = lax.axis_index("ep")
    seq = tokens_ref.shape[1]
    d_model = tokens_ref.shape[2]
    experts = wgate_ref.shape[1]
    e_loc = experts // N_DEV

    def remote(src, dst, send_sem, recv_sem, dev, mask, own):
        if mask == 0:
            pltpu.make_async_copy(src, dst, own_sem.at[own]).start()
        else:
            pltpu.make_async_remote_copy(
                src_ref=src, dst_ref=dst, send_sem=send_sem, recv_sem=recv_sem,
                device_id=(dev,), device_id_type=MESH).start()

    def send_quad(which):
        for place, mask in enumerate(ORDER):
            dev = partner(me, mask)
            row = pl.multiple_of(place * quads * FIX + which * FIX, FIX)
            remote(fix_s.at[which, dev], fix_ref.at[:, pl.ds(row, FIX), :], fix_send, fix_recv, dev, mask, 0)

    @pl.when(step == 0)
    def _():
        greet(me)
        split_gate(wgate_ref, wg_s)
        aux_s[...] = jnp.zeros_like(aux_s)
        flag_s[...] = jnp.zeros_like(flag_s)
        code_s[...] = jnp.zeros_like(code_s)
        goal_s[...] = jnp.zeros_like(goal_s)
        count_s[...] = jnp.zeros_like(count_s)

    @pl.when(step == 2)
    def _():
        pl.semaphore_wait(pltpu.get_barrier_semaphore(), N_DEV - 1)

    @pl.when((step > 0) & (lax.rem(step, 2) == 0))
    def _():
        send_quad(quad - 1)

    b, gate_probs = attend(
        step, tokens_ref, pad_ref, norm_attn_ref, wq_ref, wk_ref, wv_ref, wo_ref, norm_moe_ref, hidden_ref,
        q_s, k_s, v_s, ctx_s, s_s, p_s, wg_s, heads, head_dim, experts)
    side = lax.rem(step, 2)
    b_s[pl.ds(pl.multiple_of(side * 2 * seq, 2 * seq), 2 * seq), :] = b

    eid = lax.broadcasted_iota(jnp.int32, (experts, seq), 0)
    tri = jnp.where(lax.broadcasted_iota(jnp.int32, (seq, seq), 0) <= lax.broadcasted_iota(jnp.int32, (seq, seq), 1), 1.0, 0.0)
    tri = jnp.concatenate([tri, jnp.ones((seq, 128), F32)], axis=1).astype(BF16)
    row_e = lax.broadcasted_iota(jnp.int32, (experts, experts), 0)
    col_e = lax.broadcasted_iota(jnp.int32, (experts, experts), 1)
    same = row_e // e_loc == col_e // e_loc
    mix = jnp.concatenate([jnp.where(same & (col_e < row_e), 1.0, 0.0), jnp.where(same, 1.0, 0.0)], axis=0).astype(BF16)
    spot = lax.broadcasted_iota(jnp.int32, (experts, 128), 1).astype(F32)
    code0 = (lax.rem(lax.broadcasted_iota(jnp.int32, (experts, 128), 0), e_loc) * EXTRA + 1).astype(F32)
    meta_row = lax.broadcasted_iota(jnp.int32, (8, seq), 0)
    for grp in range(2):
        p = gate_probs[:, grp * seq:(grp + 1) * seq]
        valid = pad_ref[pl.ds(2 * step + grp, 1), :] == 1
        draw = draw_ref[pl.ds(2 * step + grp, 1), :]
        e1 = choices_ref[grp, 0:1, :]
        e2 = choices_ref[grp, 1:2, :]
        hot1 = eid == e1
        hot2 = eid == e2
        p1 = jnp.sum(jnp.where(hot1, p, 0.0), axis=0, keepdims=True)
        p2 = jnp.sum(jnp.where(hot2, p, 0.0), axis=0, keepdims=True)
        g1 = p1 / (p1 + p2)
        g2 = p2 / (p1 + p2)
        want2 = valid & (draw < 2.0 * g2)
        take1 = jnp.where(hot1 & valid, 1.0, 0.0)
        take2 = jnp.where(hot2 & want2, 1.0, 0.0)
        cum = dot(jnp.concatenate([take1, take2], axis=0).astype(BF16), tri)
        cum1 = cum[:experts, :seq]
        cum2 = cum[experts:, :seq]
        count1 = cum[:experts, seq:]
        count2 = cum[experts:, seq:]
        first = jnp.minimum(count1, float(capacity))
        pos1 = jnp.sum((cum1 - 1.0) * take1, axis=0, keepdims=True)
        pos2 = jnp.sum((cum2 - 1.0 + twice(first)) * take2, axis=0, keepdims=True)
        keep1 = valid & (pos1 < capacity)
        keep2 = want2 & (pos2 < capacity)

        share = jnp.where(valid, p, 0.0) * twice(count1 * (1.0 / (seq * seq)))
        share = jnp.sum(share.reshape(experts // 8, 8, seq), axis=0)
        for col in range(seq // 128):
            aux_s[...] += share[:, col * 128:(col + 1) * 128]

        before = count_s[0]
        after = before + jnp.minimum(first + count2, float(capacity))
        new = jnp.maximum(after - FIX, 0.0) - jnp.maximum(before - FIX, 0.0)
        sums = dot(mix, new.astype(BF16))
        packed = count_s[1]
        begin = packed + sums[:experts]
        shift = begin - jnp.maximum(before, float(FIX)) + before
        local = shift - count_s[3]
        inside = (spot >= begin) & (spot < begin + new)
        code = jnp.where(inside, code0 + count_s[2] + spot - begin, 0.0)
        code_s[...] += jnp.sum(code.reshape(N_DEV, e_loc, 128), axis=1)
        count_s[0] = after
        count_s[1] = packed + sums[experts:]
        count_s[2] += new

        def places(e, take, pos, keep):
            index = pos + jnp.sum(twice(before) * take, axis=0, keepdims=True)
            in_pack = pos + jnp.sum(twice(shift) * take, axis=0, keepdims=True)
            in_local = pos + jnp.sum(twice(local) * take, axis=0, keepdims=True)
            e = e.astype(F32)
            dev = jnp.floor(e * (1.0 / e_loc))
            fixed = keep & (index < FIX)
            loose = keep & (index >= FIX)
            at_fix = jnp.where(fixed, e * FIX + index, -1.0)
            at_local = jnp.where(loose, dev * LOCAL + in_local, -1.0)
            at_back = jnp.where(loose, experts * FIX + dev * PACK + in_pack, at_fix)
            return at_fix, at_local, at_back, jnp.where(keep, e * capacity + pos, -1.0)

        f1, l1, c1, w1 = places(e1, take1, pos1, keep1)
        f2, l2, c2, w2 = places(e2, take2, pos2, keep2)
        meta = jnp.where(meta_row == 0, c1, 0.0)
        meta = jnp.where(meta_row == 1, c2, meta)
        meta = jnp.where(meta_row == 2, g1, meta)
        meta = jnp.where(meta_row == 3, g2, meta)
        meta = jnp.where(meta_row == 4, w1, meta)
        meta = jnp.where(meta_row == 5, w2, meta)
        meta_ref[grp] = meta
        tok = pl.ds(pl.multiple_of(side * 2 * seq + grp * seq, seq), seq)
        slot_s[:, tok] = jnp.where(meta_row == 0, f1, jnp.where(meta_row == 1, f2, jnp.where(meta_row == 2, l1, l2))).astype(jnp.int32)

    @pl.when(side == 1)
    def _():
        def gather(first_row, base, count, skip):
            ids = lax.broadcasted_iota(jnp.int32, (count, 4 * seq - skip), 0) + base
            hit = (ids == slot_s[first_row:first_row + 1, skip:]) | (ids == slot_s[first_row + 1:first_row + 2, skip:])
            return dot(jnp.where(hit, 1.0, 0.0).astype(BF16), b_s[skip:, :]).astype(BF16)

        per_dev = e_loc * FIX
        for base in range(0, N_DEV, 4):
            rows = gather(0, base * per_dev, 4 * per_dev, 0)
            fix_s[quad, base:base + 4] = rows.reshape(4, e_loc, FIX, d_model)
        for base in range(0, N_DEV, 4):
            rows = gather(2, base * LOCAL, 4 * LOCAL, 2 * seq)
            local_s[base:base + 4, pl.ds(pl.multiple_of(quad * LOCAL, LOCAL), LOCAL), :] = rows.reshape(4, LOCAL, d_model)

        def per_device(value):
            return value.reshape(N_DEV, e_loc, 128)[:, 0, :]

        start = per_device(count_s[3])
        filled = per_device(count_s[1]) - start
        at = lax.broadcasted_iota(jnp.int32, (N_DEV, 256), 1).astype(F32) - (quad * LOCAL).astype(F32)
        live = (at >= 0.0) & (at < float(LOCAL)) & (at < twice(filled))
        goal_s[...] = jnp.where(live, twice(start) + at + 1.0, goal_s[...])
        flag_s[...] = jnp.maximum(flag_s[...], jnp.where(filled > LOCAL, 1.0, 0.0))
        count_s[0] = jnp.zeros_like(count_s[0])
        count_s[3] = count_s[1]

    @pl.when(step == steps - 1)
    def _():
        send_quad(quads - 1)
        width = goal_s.shape[1] * 3 // 4
        rows = lax.broadcasted_iota(jnp.int32, (PACK, width), 0).astype(F32) + 1.0
        for dev in range(N_DEV):
            hit = jnp.where(rows == goal_s[dev:dev + 1, 0:width], 1.0, 0.0).astype(BF16)
            pack_s[dev] = dot(hit, local_s[dev]).astype(BF16)
        over = jnp.where((count_s[1] > PACK) | (count_s[2] > EXTRA), 1.0, 0.0)
        over = jnp.max(jnp.max(over.reshape(N_DEV, e_loc, 128), axis=1), axis=0, keepdims=True)
        over = jnp.maximum(over, jnp.max(flag_s[...], axis=0, keepdims=True))
        tally = count_s[2].T[0:1, :]
        for dev in range(N_DEV):
            msg_s[dev, 0:8] = aux_s[...]
            lower = lax.broadcasted_iota(jnp.int32, (8, 128), 0)
            msg_s[dev, 8:16] = jnp.where(lower == 0, code_s[dev:dev + 1, :], jnp.where(lower == 1, over, jnp.where(lower == 2, tally, 0.0)))
        for place, mask in enumerate(ORDER):
            dev = partner(me, mask)
            remote(pack_s.at[dev], pack_ref.at[place], pack_send, pack_recv, dev, mask, 1)
        for place, mask in enumerate(ORDER):
            dev = partner(me, mask)
            remote(msg_s.at[dev], msg_ref.at[place], msg_send, msg_recv, dev, mask, 2)

        def settle(ref, sem):
            pltpu.make_async_copy(ref, ref, sem).wait()

        others = pl.ds(0, N_DEV - 1)
        settle(fix_s.at[:, 0], own_sem.at[0])
        settle(pack_s.at[0], own_sem.at[1])
        settle(msg_s.at[0], own_sem.at[2])
        settle(fix_s.at[:, others], fix_send)
        settle(pack_s.at[others], pack_send)
        settle(msg_s.at[others], msg_send)
        settle(fix_ref.at[:, pl.ds(0, (N_DEV - 1) * quads * FIX), :], fix_recv)
        settle(pack_ref.at[others], pack_recv)
        settle(msg_ref.at[others], msg_recv)


def packed_expert_kernel(
    fix_ref, pack_ref, msg_ref, w_in_ref, w_out_ref, back_ref, back_pack_ref,
    act_s, x_s, z_s, zx_s, code_s, pack_s, fix_send, fix_recv, pack_send, pack_recv, own_sem,
):
    e = pl.program_id(0)
    n_exp = pl.num_programs(0)
    me = lax.axis_index("ep")
    rows = fix_ref.shape[1]
    d_model = fix_ref.shape[2]
    ff = w_in_ref.shape[2]
    per_src = rows // N_DEV
    chunk = 1024

    def mlp(x):
        for f in range(ff // chunk):
            act = dot(x, w_in_ref[0, :, pl.ds(f * chunk, chunk)])
            act_s[0:x.shape[0], pl.ds(f * chunk, chunk)] = jnp.maximum(act, 0.0).astype(BF16)
        return dot(act_s[0:x.shape[0], :], w_out_ref[0]).astype(BF16)

    def spread(place):
        ids = lax.broadcasted_iota(jnp.int32, (x_s.shape[0] * POOL, PACK), 0).astype(F32) + 1.0
        return jnp.where(ids == code_s[place:place + 1, 0:PACK], 1.0, 0.0).astype(BF16)

    def remote(src, dst, send_sem, recv_sem, mask, own):
        if mask == 0:
            pltpu.make_async_copy(src, dst, own_sem.at[own]).start()
        else:
            pltpu.make_async_remote_copy(
                src_ref=src, dst_ref=dst, send_sem=send_sem, recv_sem=recv_sem,
                device_id=(partner(me, mask),), device_id_type=MESH).start()

    @pl.when(e == 0)
    def _():
        greet(me)

    z_s[e] = mlp(fix_ref[0])

    @pl.when(e == 0)
    def _():
        pl.semaphore_wait(pltpu.get_barrier_semaphore(), N_DEV - 1)

    for place, mask in enumerate(ORDER):
        remote(z_s.at[e, pl.ds(place * per_src, per_src), :], back_ref.at[me * n_exp + e], fix_send, fix_recv, mask, 0)

    @pl.when(e == 0)
    def _():
        code = jnp.concatenate([msg_ref[place, 8:9, :] for place in range(N_DEV)], axis=0)
        n_loc = x_s.shape[0]
        hits = [(code > ex * EXTRA) & (code <= (ex + 1) * EXTRA) for ex in range(n_loc)]
        row = lax.broadcasted_iota(jnp.int32, (N_DEV, N_DEV), 0)
        col = lax.broadcasted_iota(jnp.int32, (N_DEV, N_DEV), 1)
        prior = jnp.where((row // TEAM == col // TEAM) & (col < row), 1.0, 0.0).astype(BF16)
        spans = dot(prior, jnp.concatenate([jnp.where(hit, 1.0, 0.0) for hit in hits], axis=1).astype(BF16))
        shared = jnp.zeros_like(code)
        for ex, hit in enumerate(hits):
            begin = jnp.sum(spans[:, ex * 128:(ex + 1) * 128], axis=1, keepdims=True)
            shared = jnp.where(hit, code + begin + float(ex * (POOL - EXTRA)), shared)
        code_s[...] = shared
        for team in range(N_DEV // TEAM):
            x = dot(spread(team * TEAM), pack_ref[team * TEAM])
            for place in range(team * TEAM + 1, (team + 1) * TEAM):
                x = x + dot(spread(place), pack_ref[place])
            x_s[:, pl.ds(team * POOL, POOL), :] = x.astype(BF16).reshape(n_loc, POOL, d_model)

    zx_s[e] = mlp(x_s[e])

    @pl.when(e == n_exp - 1)
    def _():
        for place, mask in enumerate(ORDER):
            z = zx_s[:, pl.ds(place // TEAM * POOL, POOL), :].reshape(x_s.shape[0] * POOL, d_model)
            pack_s[place] = lax.dot_general(
                spread(place), z, (((0,), (0,)), ((), ())), preferred_element_type=F32).astype(BF16)
            if place > 0:
                remote(pack_s.at[place - 1], back_pack_ref.at[me], pack_send, pack_recv, ORDER[place - 1], 1)
        remote(pack_s.at[N_DEV - 1], back_pack_ref.at[me], pack_send, pack_recv, ORDER[N_DEV - 1], 1)

        def settle(ref, sem):
            pltpu.make_async_copy(ref, ref, sem).wait()

        others = pl.ds(0, N_DEV - 1)
        settle(z_s.at[:, pl.ds(0, per_src), :], own_sem.at[0])
        settle(pack_s.at[0], own_sem.at[1])
        settle(z_s.at[:, pl.ds(0, (N_DEV - 1) * per_src), :], fix_send)
        settle(pack_s.at[others], pack_send)
        settle(back_ref.at[pl.ds(0, (N_DEV - 1) * n_exp)], fix_recv)
        settle(back_pack_ref.at[others], pack_recv)


def packed_back_kernel(fix_ref, pack_ref, hidden_ref, meta_ref, msg_ref, out_ref, aux_ref, *, n_groups):
    experts, rows, d_model = fix_ref.shape
    seq = hidden_ref.shape[1]
    z = fix_ref[...].reshape(experts * rows, d_model)
    zx = pack_ref[...].reshape(N_DEV * PACK, d_model)
    fix_id = lax.broadcasted_iota(jnp.int32, (seq, experts * rows), 1)
    pack_id = lax.broadcasted_iota(jnp.int32, (seq, N_DEV * PACK), 1) + experts * rows
    for grp in range(2):
        meta = meta_ref[grp].T
        c1 = meta[:, 0:1].astype(jnp.int32)
        c2 = meta[:, 1:2].astype(jnp.int32)
        g1 = meta[:, 2:3]
        g2 = meta[:, 3:4]

        def gates(ids):
            return jnp.where(ids == c1, g1, jnp.where(ids == c2, g2, 0.0)).astype(BF16)

        moe = dot(gates(fix_id), z) + dot(gates(pack_id), zx)
        out_ref[grp] = (hidden_ref[grp].astype(F32) + moe).astype(BF16)

    @pl.when(pl.program_id(0) == 0)
    def _():
        total = jnp.sum(msg_ref[:, 0:8, :], axis=0)
        total = jnp.sum(jnp.sum(total, axis=1, keepdims=True), axis=0, keepdims=True)
        aux_ref[...] = jnp.broadcast_to(total * (experts / n_groups), aux_ref.shape)


def solution(mesh):
    def local_step(tokens, pad_mask, second_draw, choices, norm_attn, w_query, w_key, w_value, w_attn_out, norm_moe, w_gate, w_in, w_out):
        groups, seq, d_model = tokens.shape
        _, heads, head_dim = w_query.shape
        experts = w_gate.shape[1]
        ff = w_in.shape[2]
        e_loc = experts // N_DEV
        capacity = (2 * seq + experts - 1) // experts
        hw = heads * head_dim
        rows = 2 * capacity
        steps = groups // 2
        all_rows = N_DEV * steps * rows

        wq, wk, wv = (w.transpose(1, 2, 0).reshape(hw, d_model) for w in (w_query, w_key, w_value))
        wo = w_attn_out.reshape(hw, d_model)

        def whole(shape):
            return pl.BlockSpec(shape, lambda i: (0,) * len(shape), pipeline_mode=pl.Buffered(1))

        anywhere = pl.BlockSpec(memory_space=pl.ANY)
        front_specs = [
            pl.BlockSpec((2, seq, d_model), lambda i: (i, 0, 0)),
            whole((groups, seq)), whole((groups, seq)),
            pl.BlockSpec((2, 2, seq), lambda i: (i, 0, 0)),
            whole((d_model,)), whole((hw, d_model)), whole((hw, d_model)), whole((hw, d_model)), whole((hw, d_model)),
            whole((d_model,)), whole((d_model, experts)),
        ]
        quads = steps // 2
        fix_rows = quads * FIX
        dma = pltpu.SemaphoreType.DMA
        hidden_p, meta_p, fix, pack, msg = pl.pallas_call(
            functools.partial(packed_front_kernel, heads=heads, head_dim=head_dim, capacity=capacity),
            name="packed_front",
            grid=(steps,),
            in_specs=front_specs,
            out_specs=[
                pl.BlockSpec((2, seq, d_model), lambda i: (i, 0, 0)),
                pl.BlockSpec((2, 8, seq), lambda i: (i, 0, 0)),
                anywhere, anywhere, anywhere,
            ],
            out_shape=[
                jax.ShapeDtypeStruct((groups, seq, d_model), BF16),
                jax.ShapeDtypeStruct((groups, 8, seq), F32),
                jax.ShapeDtypeStruct((e_loc, N_DEV * fix_rows, d_model), BF16),
                jax.ShapeDtypeStruct((N_DEV, PACK, d_model), BF16),
                jax.ShapeDtypeStruct((N_DEV, 16, 128), F32),
            ],
            scratch_shapes=[
                pltpu.VMEM((hw, 2 * seq), BF16),
                pltpu.VMEM((2 * seq, hw), BF16),
                pltpu.VMEM((hw, 2 * seq), BF16),
                pltpu.VMEM((hw, 2 * seq), BF16),
                pltpu.VMEM((2, 4, seq, seq), F32),
                pltpu.VMEM((2, 4, seq, seq), BF16),
                pltpu.VMEM((3 * experts, d_model), BF16),
                pltpu.VMEM((4 * seq, d_model), BF16),
                pltpu.VMEM((8, 4 * seq), jnp.int32),
                pltpu.VMEM((4, experts, 128), F32),
                pltpu.VMEM((8, 128), F32),
                pltpu.VMEM((N_DEV, 128), F32),
                pltpu.VMEM((N_DEV, 128), F32),
                pltpu.VMEM((N_DEV, 256), F32),
                pltpu.VMEM((N_DEV, quads * LOCAL, d_model), BF16),
                pltpu.VMEM((quads, N_DEV, e_loc, FIX, d_model), BF16),
                pltpu.VMEM((N_DEV, PACK, d_model), BF16),
                pltpu.VMEM((N_DEV, 16, 128), F32),
                dma, dma, dma, dma, dma, dma, dma((3,)),
            ],
            compiler_params=pltpu.CompilerParams(
                dimension_semantics=("arbitrary",), collective_id=0, has_side_effects=True, vmem_limit_bytes=VMEM_LIMIT),
        )(tokens, pad_mask, second_draw, choices.transpose(0, 2, 1), norm_attn, wq, wk, wv, wo, norm_moe, w_gate)

        def packed_path():
            back, back_pack = pl.pallas_call(
                packed_expert_kernel,
                name="packed_experts",
                grid=(e_loc,),
                in_specs=[
                    pl.BlockSpec((1, N_DEV * fix_rows, d_model), lambda i: (i, 0, 0)),
                    whole((N_DEV, PACK, d_model)), whole((N_DEV, 16, 128)),
                    pl.BlockSpec((1, d_model, ff), lambda i: (i, 0, 0)),
                    pl.BlockSpec((1, ff, d_model), lambda i: (i, 0, 0)),
                ],
                out_specs=[anywhere, anywhere],
                out_shape=[
                    jax.ShapeDtypeStruct((experts, fix_rows, d_model), BF16),
                    jax.ShapeDtypeStruct((N_DEV, PACK, d_model), BF16),
                ],
                scratch_shapes=[
                    pltpu.VMEM((N_DEV * fix_rows, ff), BF16),
                    pltpu.VMEM((e_loc, N_DEV // TEAM * POOL, d_model), BF16),
                    pltpu.VMEM((e_loc, N_DEV * fix_rows, d_model), BF16),
                    pltpu.VMEM((e_loc, N_DEV // TEAM * POOL, d_model), BF16),
                    pltpu.VMEM((N_DEV, 128), F32),
                    pltpu.VMEM((N_DEV, PACK, d_model), BF16),
                    dma, dma, dma, dma, dma((2,)),
                ],
                compiler_params=pltpu.CompilerParams(
                    dimension_semantics=("arbitrary",), collective_id=1, has_side_effects=True, vmem_limit_bytes=VMEM_LIMIT),
            )(fix, pack, msg, w_in, w_out)
            return pl.pallas_call(
                functools.partial(packed_back_kernel, n_groups=groups * N_DEV),
                name="packed_back",
                grid=(steps,),
                in_specs=[
                    pl.BlockSpec((experts, FIX, d_model), lambda i: (0, i // 2, 0)),
                    whole((N_DEV, PACK, d_model)),
                    pl.BlockSpec((2, seq, d_model), lambda i: (i, 0, 0)),
                    pl.BlockSpec((2, 8, seq), lambda i: (i, 0, 0)),
                    whole((N_DEV, 16, 128)),
                ],
                out_specs=[
                    pl.BlockSpec((2, seq, d_model), lambda i: (i, 0, 0)),
                    pl.BlockSpec((8, 128), lambda i: (0, 0)),
                ],
                out_shape=[
                    jax.ShapeDtypeStruct((groups, seq, d_model), BF16),
                    jax.ShapeDtypeStruct((8, 128), F32),
                ],
                compiler_params=pltpu.CompilerParams(dimension_semantics=("arbitrary",), vmem_limit_bytes=VMEM_LIMIT),
            )(back, back_pack, hidden_p, meta_p, msg)

        def full_path():
            recv = pl.pallas_call(
                functools.partial(full_front_kernel, experts=experts, capacity=capacity),
                name="full_front",
                grid=(steps,),
                in_specs=[
                    pl.BlockSpec((2, seq, d_model), lambda i: (i, 0, 0)),
                    pl.BlockSpec((2, 8, seq), lambda i: (i, 0, 0)),
                    whole((d_model,)),
                ],
                out_specs=anywhere,
                out_shape=jax.ShapeDtypeStruct((e_loc, all_rows, d_model), BF16),
                scratch_shapes=[pltpu.VMEM((steps, N_DEV, e_loc, rows, d_model), BF16), dma, dma, dma],
                compiler_params=pltpu.CompilerParams(
                    dimension_semantics=("arbitrary",), collective_id=2, has_side_effects=True, vmem_limit_bytes=VMEM_LIMIT),
            )(hidden_p, meta_p, norm_moe)
            tile = all_rows // 4
            ret = pl.pallas_call(
                functools.partial(expert_kernel, tile=tile),
                name="full_experts",
                grid=(e_loc,),
                in_specs=[
                    pl.BlockSpec((1, all_rows, d_model), lambda i: (i, 0, 0)),
                    pl.BlockSpec((1, d_model, ff), lambda i: (i, 0, 0)),
                    pl.BlockSpec((1, ff, d_model), lambda i: (i, 0, 0)),
                ],
                out_specs=anywhere,
                out_shape=jax.ShapeDtypeStruct((experts, steps * rows, d_model), BF16),
                scratch_shapes=[pltpu.VMEM((tile, ff), BF16), pltpu.VMEM((e_loc, all_rows, d_model), BF16), dma, dma, dma],
                compiler_params=pltpu.CompilerParams(
                    dimension_semantics=("arbitrary",), collective_id=3, has_side_effects=True, vmem_limit_bytes=VMEM_LIMIT),
            )(recv, w_in, w_out)
            return pl.pallas_call(
                functools.partial(back_kernel, n_groups=groups * N_DEV, capacity=capacity),
                name="full_back",
                grid=(steps,),
                in_specs=[
                    pl.BlockSpec((experts, rows, d_model), lambda i: (0, i, 0)),
                    pl.BlockSpec((2, seq, d_model), lambda i: (i, 0, 0)),
                    pl.BlockSpec((2, 8, seq), lambda i: (i, 0, 0)),
                    whole((N_DEV, 16, 128)),
                ],
                out_specs=[
                    pl.BlockSpec((2, seq, d_model), lambda i: (i, 0, 0)),
                    pl.BlockSpec((8, 128), lambda i: (0, 0)),
                ],
                out_shape=[
                    jax.ShapeDtypeStruct((groups, seq, d_model), BF16),
                    jax.ShapeDtypeStruct((8, 128), F32),
                ],
                compiler_params=pltpu.CompilerParams(dimension_semantics=("arbitrary",), vmem_limit_bytes=VMEM_LIMIT),
            )(ret, hidden_p, meta_p, msg)

        shared = jnp.sum(msg[:, 10, :].reshape(N_DEV // TEAM, TEAM, experts), axis=1)
        spilled = (jnp.max(msg[:, 9, 0]) > 0.0) | (jnp.max(shared) > POOL)
        out, aux = lax.cond(spilled, full_path, packed_path)
        return out, aux[0, 0]

    by_group = P("ep")
    replicated = P()
    in_specs = (by_group, by_group, by_group, by_group, replicated, replicated, replicated, replicated, replicated, replicated, replicated, by_group, by_group)
    return jax.shard_map(local_step, mesh=mesh, in_specs=in_specs, out_specs=(by_group, replicated), check_vma=False)
```

profile of v0, /device:TPU:1, one launch (start us, length us, event | category | flops | bytes accessed | tf_op | source)
XLA Modules:
  0.0 285.2 jit_solution(11246868023879548113)
XLA Ops:
  0.6 0.0 copy-start
  0.6 133.6 %packed_front.1 = (bf16[16,256,768]{2,1,0:T(8,128)(2,1)}, f32[16,8,256]{2,1,0:T(8,128)S(1)}, bf16[8,512,768]{2,1,0:T(8,128)(2,1)}, bf16[16,112,768]{2,1,0:T(8,128)(2,1)}, f32[16,16,128]{2,1,0:T(8,128)S(1)}) custom-call(bf16[16,256,768]{2,1,0:T(8,128)(2,1)} %tokens_ref.1, s32[16,256]{1,0:T(8,128)} %pad_ref.1, f32[16,256]{1,0:T(8,128)} %draw_ref.1, ...), custom_call_target="tpu_custom_call" | custom-call | tf_op jit(solution)/shard_map/packed_front/pallas_call | solution.py:621
  134.2 0.6 slice_reduce_fusion
  135.5 0.6 reduce_max.19
  136.8 0.0 copy-done
  136.8 148.4 %conditional.1 = (bf16[16,256,768]{2,1,0:T(8,128)(2,1)}, f32[]{:T(128)}) conditional(s32[]{:T(128)} %convert_element_type.3, (bf16[8,512,768]{2,1,0:T(8,128)(2,1)}, bf16[16,112,768]{2,1,0:T(8,128)(2,1)}, f32[16,16,128]{2,1,0:T(8,128)S(1)}, bf16[8,768,3072]{2,1,0:T(8,128)(2,1)}, bf16[8,3072,768]{2,1,0:T(8,128)(2,1)}, ...), branch_computations={%region_3.0_spmd, %region_4.0_spmd} | conditional | bytes 24 | solution.py:768
  136.8 121.6 %packed_experts.1 = (bf16[128,32,768]{2,1,0:T(8,128)(2,1)}, bf16[16,112,768]{2,1,0:T(8,128)(2,1)}) custom-call(bf16[8,512,768]{2,1,0:T(8,128)(2,1)} %get-tuple-element.31.fix_ref, bf16[16,112,768]{2,1,0:T(8,128)(2,1)} %get-tuple-element.32.pack_ref, f32[16,16,128]{2,1,0:T(8,128)S(1)} %get-tuple-element.33.msg_ref, ...), custom_call_target="tpu_custom_call" | custom-call | tf_op jit(solution)/shard_map/cond/branch_0_fun/packed_experts/pallas_call | solution.py:664
  258.4 25.7 %packed_back.1 = (bf16[16,256,768]{2,1,0:T(8,128)(2,1)}, f32[8,128]{1,0:T(8,128)}) custom-call(bf16[128,32,768]{2,1,0:T(8,128)(2,1)} %get-tuple-element.36.fix_ref, bf16[16,112,768]{2,1,0:T(8,128)(2,1)} %get-tuple-element.37.pack_ref, bf16[16,256,768]{2,1,0:T(8,128)(2,1)} %get-tuple-element.38.hidden_ref, f32[16,8,256]{2,1,0:T(8,128)S(1)} %get-tuple-element.39.meta_ref, ...), custom_call_target="tpu_custom_call" | custom-call | tf_op jit(solution)/shard_map/cond/branch_0_fun/packed_back/pallas_call | solution.py:691
  284.0 1.2 slice.9
  (2 shorter events, 0.0 us)
Async XLA Ops:
  0.6 136.1 %copy-start = (f32[768]{0:T(1024)S(1)}, f32[768]{0:T(1024)}, u32[]{:S(2)}) copy-start(f32[768]{0:T(1024)} %norm_moe_ref.1) | copy-start | bytes 9220
where the time goes:
time: 285 us
  Pallas kernels  281 us (99%)
    pallas_call x1, Pallas kernels, local_step(): pl.pallas_call(functools.partial(packed_front_kernel, heads=heads, head_d...  134 us
    pallas_call x1, Pallas kernels, packed_path(): pl.pallas_call(packed_expert_kernel, name='packed_experts', grid=(e_loc,)...  122 us
    pallas_call x1, Pallas kernels, packed_path(): pl.pallas_call(functools.partial(packed_back_kernel, n_groups=groups * N_...  25.7 us

commit v1 on v0

--- a/solution.py
+++ b/solution.py
@@ -255,9 +255,7 @@
 
     @pl.when(pl.program_id(0) == 0)
     def _():
-        total = jnp.sum(msg_ref[:, 0:8, :], axis=0)
-        total = jnp.sum(jnp.sum(total, axis=1, keepdims=True), axis=0, keepdims=True)
-        aux_ref[...] = jnp.broadcast_to(total * (experts / n_groups), aux_ref.shape)
+        aux_ref[0, 0] = jnp.sum(msg_ref[:, 0:8, :]) * (experts / n_groups)
 
 
 FIX = 8
@@ -266,6 +264,7 @@
 EXTRA = 32
 TEAM = 4
 POOL = 80
+WINDOW = 64
 
 
 def twice(value):
@@ -274,9 +273,9 @@
 
 def packed_front_kernel(
     tokens_ref, pad_ref, draw_ref, choices_ref, norm_attn_ref, wq_ref, wk_ref, wv_ref, wo_ref, norm_moe_ref, wgate_ref,
-    hidden_ref, meta_ref, fix_ref, pack_ref, msg_ref,
+    hidden_ref, meta_ref, pack_s, starts_ref, fix_ref, msg_ref,
     q_s, k_s, v_s, ctx_s, s_s, p_s, wg_s, b_s, slot_s, count_s, aux_s, flag_s, code_s, goal_s,
-    local_s, fix_s, pack_s, msg_s, fix_send, fix_recv, pack_send, pack_recv, msg_send, msg_recv, own_sem,
+    local_s, fix_s, msg_s, fix_send, fix_recv, msg_send, msg_recv, own_sem,
     *, heads, head_dim, capacity,
 ):
     step = pl.program_id(0)
@@ -337,6 +336,10 @@
     spot = lax.broadcasted_iota(jnp.int32, (experts, 128), 1).astype(F32)
     code0 = (lax.rem(lax.broadcasted_iota(jnp.int32, (experts, 128), 0), e_loc) * EXTRA + 1).astype(F32)
     meta_row = lax.broadcasted_iota(jnp.int32, (8, seq), 0)
+
+    def window_start():
+        return jnp.minimum(jnp.floor(count_s[3] * (1.0 / 16)) * 16.0, float(PACK - WINDOW))
+
     for grp in range(2):
         p = gate_probs[:, grp * seq:(grp + 1) * seq]
         valid = pad_ref[pl.ds(2 * step + grp, 1), :] == 1
@@ -376,6 +379,7 @@
         begin = packed + sums[:experts]
         shift = begin - jnp.maximum(before, float(FIX)) + before
         local = shift - count_s[3]
+        window = shift - window_start()
         inside = (spot >= begin) & (spot < begin + new)
         code = jnp.where(inside, code0 + count_s[2] + spot - begin, 0.0)
         code_s[...] += jnp.sum(code.reshape(N_DEV, e_loc, 128), axis=1)
@@ -385,7 +389,7 @@
 
         def places(e, take, pos, keep):
             index = pos + jnp.sum(twice(before) * take, axis=0, keepdims=True)
-            in_pack = pos + jnp.sum(twice(shift) * take, axis=0, keepdims=True)
+            in_window = pos + jnp.sum(twice(window) * take, axis=0, keepdims=True)
             in_local = pos + jnp.sum(twice(local) * take, axis=0, keepdims=True)
             e = e.astype(F32)
             dev = jnp.floor(e * (1.0 / e_loc))
@@ -393,7 +397,7 @@
             loose = keep & (index >= FIX)
             at_fix = jnp.where(fixed, e * FIX + index, -1.0)
             at_local = jnp.where(loose, dev * LOCAL + in_local, -1.0)
-            at_back = jnp.where(loose, experts * FIX + dev * PACK + in_pack, at_fix)
+            at_back = jnp.where(loose, experts * FIX + dev * WINDOW + in_window, at_fix)
             return at_fix, at_local, at_back, jnp.where(keep, e * capacity + pos, -1.0)
 
         f1, l1, c1, w1 = places(e1, take1, pos1, keep1)
@@ -432,17 +436,13 @@
         live = (at >= 0.0) & (at < float(LOCAL)) & (at < twice(filled))
         goal_s[...] = jnp.where(live, twice(start) + at + 1.0, goal_s[...])
         flag_s[...] = jnp.maximum(flag_s[...], jnp.where(filled > LOCAL, 1.0, 0.0))
+        starts_ref[pl.ds(quad, 1), :] = window_start().T[0:1, :].astype(jnp.int32)
         count_s[0] = jnp.zeros_like(count_s[0])
         count_s[3] = count_s[1]
 
     @pl.when(step == steps - 1)
     def _():
         send_quad(quads - 1)
-        width = goal_s.shape[1] * 3 // 4
-        rows = lax.broadcasted_iota(jnp.int32, (PACK, width), 0).astype(F32) + 1.0
-        for dev in range(N_DEV):
-            hit = jnp.where(rows == goal_s[dev:dev + 1, 0:width], 1.0, 0.0).astype(BF16)
-            pack_s[dev] = dot(hit, local_s[dev]).astype(BF16)
         over = jnp.where((count_s[1] > PACK) | (count_s[2] > EXTRA), 1.0, 0.0)
         over = jnp.max(jnp.max(over.reshape(N_DEV, e_loc, 128), axis=1), axis=0, keepdims=True)
         over = jnp.maximum(over, jnp.max(flag_s[...], axis=0, keepdims=True))
@@ -453,32 +453,33 @@
             msg_s[dev, 8:16] = jnp.where(lower == 0, code_s[dev:dev + 1, :], jnp.where(lower == 1, over, jnp.where(lower == 2, tally, 0.0)))
         for place, mask in enumerate(ORDER):
             dev = partner(me, mask)
-            remote(pack_s.at[dev], pack_ref.at[place], pack_send, pack_recv, dev, mask, 1)
-        for place, mask in enumerate(ORDER):
-            dev = partner(me, mask)
-            remote(msg_s.at[dev], msg_ref.at[place], msg_send, msg_recv, dev, mask, 2)
+            remote(msg_s.at[dev], msg_ref.at[place], msg_send, msg_recv, dev, mask, 1)
+
+        width = goal_s.shape[1] * 3 // 4
+        rows = lax.broadcasted_iota(jnp.int32, (PACK, width), 0).astype(F32) + 1.0
+        for dev in range(N_DEV):
+            hit = jnp.where(rows == goal_s[dev:dev + 1, 0:width], 1.0, 0.0).astype(BF16)
+            pack_s[dev] = dot(hit, local_s[dev]).astype(BF16)
 
         def settle(ref, sem):
             pltpu.make_async_copy(ref, ref, sem).wait()
 
         others = pl.ds(0, N_DEV - 1)
         settle(fix_s.at[:, 0], own_sem.at[0])
-        settle(pack_s.at[0], own_sem.at[1])
-        settle(msg_s.at[0], own_sem.at[2])
+        settle(msg_s.at[0], own_sem.at[1])
         settle(fix_s.at[:, others], fix_send)
-        settle(pack_s.at[others], pack_send)
         settle(msg_s.at[others], msg_send)
         settle(fix_ref.at[:, pl.ds(0, (N_DEV - 1) * quads * FIX), :], fix_recv)
-        settle(pack_ref.at[others], pack_recv)
         settle(msg_ref.at[others], msg_recv)
 
 
 def packed_expert_kernel(
-    fix_ref, pack_ref, msg_ref, w_in_ref, w_out_ref, back_ref, back_pack_ref,
-    act_s, x_s, z_s, zx_s, code_s, pack_s, fix_send, fix_recv, pack_send, pack_recv, own_sem,
+    fix_ref, mine_ref, msg_ref, w_in_ref, w_out_ref, back_ref, back_pack_ref,
+    act_s, x_s, z_s, zx_s, code_s, pack_ref, pack_s, in_send, in_recv, fix_send, fix_recv, pack_send, pack_recv, own_sem,
 ):
-    e = pl.program_id(0)
-    n_exp = pl.num_programs(0)
+    step = pl.program_id(0)
+    n_exp = pl.num_programs(0) // 2
+    e = lax.rem(step, n_exp)
     me = lax.axis_index("ep")
     rows = fix_ref.shape[1]
     d_model = fix_ref.shape[2]
@@ -504,21 +505,28 @@
                 src_ref=src, dst_ref=dst, send_sem=send_sem, recv_sem=recv_sem,
                 device_id=(partner(me, mask),), device_id_type=MESH).start()
 
-    @pl.when(e == 0)
+    def settle(ref, sem):
+        pltpu.make_async_copy(ref, ref, sem).wait()
+
+    others = pl.ds(0, N_DEV - 1)
+
+    @pl.when(step == 0)
     def _():
         greet(me)
-
-    z_s[e] = mlp(fix_ref[0])
-
-    @pl.when(e == 0)
-    def _():
         pl.semaphore_wait(pltpu.get_barrier_semaphore(), N_DEV - 1)
-
-    for place, mask in enumerate(ORDER):
-        remote(z_s.at[e, pl.ds(place * per_src, per_src), :], back_ref.at[me * n_exp + e], fix_send, fix_recv, mask, 0)
-
-    @pl.when(e == 0)
-    def _():
+        for place, mask in enumerate(ORDER):
+            remote(mine_ref.at[partner(me, mask)], pack_ref.at[place], in_send, in_recv, mask, 0)
+
+    @pl.when(step < n_exp)
+    def _():
+        z_s[e] = mlp(fix_ref[0])
+        for place, mask in enumerate(ORDER):
+            remote(z_s.at[e, pl.ds(place * per_src, per_src), :], back_ref.at[me * n_exp + e], fix_send, fix_recv, mask, 1)
+
+    @pl.when(step == n_exp)
+    def _():
+        settle(pack_ref.at[0], own_sem.at[0])
+        settle(pack_ref.at[others], in_recv)
         code = jnp.concatenate([msg_ref[place, 8:9, :] for place in range(N_DEV)], axis=0)
         n_loc = x_s.shape[0]
         hits = [(code > ex * EXTRA) & (code <= (ex + 1) * EXTRA) for ex in range(n_loc)]
@@ -537,37 +545,43 @@
                 x = x + dot(spread(place), pack_ref[place])
             x_s[:, pl.ds(team * POOL, POOL), :] = x.astype(BF16).reshape(n_loc, POOL, d_model)
 
-    zx_s[e] = mlp(x_s[e])
-
-    @pl.when(e == n_exp - 1)
+    @pl.when(step >= n_exp)
+    def _():
+        zx_s[e] = mlp(x_s[e])
+
+    @pl.when(step == 2 * n_exp - 1)
     def _():
         for place, mask in enumerate(ORDER):
             z = zx_s[:, pl.ds(place // TEAM * POOL, POOL), :].reshape(x_s.shape[0] * POOL, d_model)
             pack_s[place] = lax.dot_general(
                 spread(place), z, (((0,), (0,)), ((), ())), preferred_element_type=F32).astype(BF16)
             if place > 0:
-                remote(pack_s.at[place - 1], back_pack_ref.at[me], pack_send, pack_recv, ORDER[place - 1], 1)
-        remote(pack_s.at[N_DEV - 1], back_pack_ref.at[me], pack_send, pack_recv, ORDER[N_DEV - 1], 1)
-
-        def settle(ref, sem):
-            pltpu.make_async_copy(ref, ref, sem).wait()
-
-        others = pl.ds(0, N_DEV - 1)
-        settle(z_s.at[:, pl.ds(0, per_src), :], own_sem.at[0])
-        settle(pack_s.at[0], own_sem.at[1])
+                remote(pack_s.at[place - 1], back_pack_ref.at[me], pack_send, pack_recv, ORDER[place - 1], 2)
+        remote(pack_s.at[N_DEV - 1], back_pack_ref.at[me], pack_send, pack_recv, ORDER[N_DEV - 1], 2)
+        settle(z_s.at[:, pl.ds(0, per_src), :], own_sem.at[1])
+        settle(pack_s.at[0], own_sem.at[2])
+        settle(mine_ref.at[others], in_send)
         settle(z_s.at[:, pl.ds(0, (N_DEV - 1) * per_src), :], fix_send)
         settle(pack_s.at[others], pack_send)
         settle(back_ref.at[pl.ds(0, (N_DEV - 1) * n_exp)], fix_recv)
         settle(back_pack_ref.at[others], pack_recv)
 
 
-def packed_back_kernel(fix_ref, pack_ref, hidden_ref, meta_ref, msg_ref, out_ref, aux_ref, *, n_groups):
+def packed_back_kernel(starts_ref, fix_ref, pack_ref, hidden_ref, meta_ref, msg_ref, out_ref, aux_ref, window_s, *, n_groups):
     experts, rows, d_model = fix_ref.shape
     seq = hidden_ref.shape[1]
     z = fix_ref[...].reshape(experts * rows, d_model)
-    zx = pack_ref[...].reshape(N_DEV * PACK, d_model)
+    step = pl.program_id(0)
+
+    @pl.when(lax.rem(step, 2) == 0)
+    def _():
+        for dev in range(N_DEV):
+            start = pl.multiple_of(starts_ref[step // 2, dev * (experts // N_DEV)], 16)
+            window_s[dev * WINDOW:(dev + 1) * WINDOW, :] = pack_ref[dev, pl.ds(start, WINDOW), :]
+
+    zx = window_s[...]
     fix_id = lax.broadcasted_iota(jnp.int32, (seq, experts * rows), 1)
-    pack_id = lax.broadcasted_iota(jnp.int32, (seq, N_DEV * PACK), 1) + experts * rows
+    pack_id = lax.broadcasted_iota(jnp.int32, (seq, N_DEV * WINDOW), 1) + experts * rows
     for grp in range(2):
         meta = meta_ref[grp].T
         c1 = meta[:, 0:1].astype(jnp.int32)
@@ -583,9 +597,7 @@
 
     @pl.when(pl.program_id(0) == 0)
     def _():
-        total = jnp.sum(msg_ref[:, 0:8, :], axis=0)
-        total = jnp.sum(jnp.sum(total, axis=1, keepdims=True), axis=0, keepdims=True)
-        aux_ref[...] = jnp.broadcast_to(total * (experts / n_groups), aux_ref.shape)
+        aux_ref[0, 0] = jnp.sum(msg_ref[:, 0:8, :]) * (experts / n_groups)
 
 
 def solution(mesh):
@@ -618,7 +630,7 @@
         quads = steps // 2
         fix_rows = quads * FIX
         dma = pltpu.SemaphoreType.DMA
-        hidden_p, meta_p, fix, pack, msg = pl.pallas_call(
+        hidden_p, meta_p, mine, starts, fix, msg = pl.pallas_call(
             functools.partial(packed_front_kernel, heads=heads, head_dim=head_dim, capacity=capacity),
             name="packed_front",
             grid=(steps,),
@@ -626,13 +638,16 @@
             out_specs=[
                 pl.BlockSpec((2, seq, d_model), lambda i: (i, 0, 0)),
                 pl.BlockSpec((2, 8, seq), lambda i: (i, 0, 0)),
-                anywhere, anywhere, anywhere,
+                pl.BlockSpec((N_DEV, PACK, d_model), lambda i: (0, 0, 0)),
+                pl.BlockSpec((8, 128), lambda i: (0, 0)),
+                anywhere, anywhere,
             ],
             out_shape=[
                 jax.ShapeDtypeStruct((groups, seq, d_model), BF16),
                 jax.ShapeDtypeStruct((groups, 8, seq), F32),
+                jax.ShapeDtypeStruct((N_DEV, PACK, d_model), BF16),
+                jax.ShapeDtypeStruct((8, 128), jnp.int32),
                 jax.ShapeDtypeStruct((e_loc, N_DEV * fix_rows, d_model), BF16),
-                jax.ShapeDtypeStruct((N_DEV, PACK, d_model), BF16),
                 jax.ShapeDtypeStruct((N_DEV, 16, 128), F32),
             ],
             scratch_shapes=[
@@ -652,9 +667,8 @@
                 pltpu.VMEM((N_DEV, 256), F32),
                 pltpu.VMEM((N_DEV, quads * LOCAL, d_model), BF16),
                 pltpu.VMEM((quads, N_DEV, e_loc, FIX, d_model), BF16),
-                pltpu.VMEM((N_DEV, PACK, d_model), BF16),
                 pltpu.VMEM((N_DEV, 16, 128), F32),
-                dma, dma, dma, dma, dma, dma, dma((3,)),
+                dma, dma, dma, dma, dma((2,)),
             ],
             compiler_params=pltpu.CompilerParams(
                 dimension_semantics=("arbitrary",), collective_id=0, has_side_effects=True, vmem_limit_bytes=VMEM_LIMIT),
@@ -664,12 +678,12 @@
             back, back_pack = pl.pallas_call(
                 packed_expert_kernel,
                 name="packed_experts",
-                grid=(e_loc,),
+                grid=(2 * e_loc,),
                 in_specs=[
-                    pl.BlockSpec((1, N_DEV * fix_rows, d_model), lambda i: (i, 0, 0)),
+                    pl.BlockSpec((1, N_DEV * fix_rows, d_model), lambda i: (jnp.minimum(i, e_loc - 1), 0, 0)),
                     whole((N_DEV, PACK, d_model)), whole((N_DEV, 16, 128)),
-                    pl.BlockSpec((1, d_model, ff), lambda i: (i, 0, 0)),
-                    pl.BlockSpec((1, ff, d_model), lambda i: (i, 0, 0)),
+                    pl.BlockSpec((1, d_model, ff), lambda i: (lax.rem(i, e_loc), 0, 0)),
+                    pl.BlockSpec((1, ff, d_model), lambda i: (lax.rem(i, e_loc), 0, 0)),
                 ],
                 out_specs=[anywhere, anywhere],
                 out_shape=[
@@ -683,32 +697,37 @@
                     pltpu.VMEM((e_loc, N_DEV // TEAM * POOL, d_model), BF16),
                     pltpu.VMEM((N_DEV, 128), F32),
                     pltpu.VMEM((N_DEV, PACK, d_model), BF16),
-                    dma, dma, dma, dma, dma((2,)),
+                    pltpu.VMEM((N_DEV, PACK, d_model), BF16),
+                    dma, dma, dma, dma, dma, dma, dma((3,)),
                 ],
                 compiler_params=pltpu.CompilerParams(
                     dimension_semantics=("arbitrary",), collective_id=1, has_side_effects=True, vmem_limit_bytes=VMEM_LIMIT),
-            )(fix, pack, msg, w_in, w_out)
+            )(fix, mine, msg, w_in, w_out)
             return pl.pallas_call(
                 functools.partial(packed_back_kernel, n_groups=groups * N_DEV),
                 name="packed_back",
-                grid=(steps,),
-                in_specs=[
-                    pl.BlockSpec((experts, FIX, d_model), lambda i: (0, i // 2, 0)),
-                    whole((N_DEV, PACK, d_model)),
-                    pl.BlockSpec((2, seq, d_model), lambda i: (i, 0, 0)),
-                    pl.BlockSpec((2, 8, seq), lambda i: (i, 0, 0)),
-                    whole((N_DEV, 16, 128)),
-                ],
-                out_specs=[
-                    pl.BlockSpec((2, seq, d_model), lambda i: (i, 0, 0)),
-                    pl.BlockSpec((8, 128), lambda i: (0, 0)),
-                ],
+                grid_spec=pltpu.PrefetchScalarGridSpec(
+                    num_scalar_prefetch=1,
+                    grid=(steps,),
+                    in_specs=[
+                        pl.BlockSpec((experts, FIX, d_model), lambda i, starts: (0, i // 2, 0)),
+                        pl.BlockSpec((N_DEV, PACK, d_model), lambda i, starts: (0, 0, 0), pipeline_mode=pl.Buffered(1)),
+                        pl.BlockSpec((2, seq, d_model), lambda i, starts: (i, 0, 0)),
+                        pl.BlockSpec((2, 8, seq), lambda i, starts: (i, 0, 0)),
+                        pl.BlockSpec((N_DEV, 16, 128), lambda i, starts: (0, 0, 0), pipeline_mode=pl.Buffered(1)),
+                    ],
+                    out_specs=[
+                        pl.BlockSpec((2, seq, d_model), lambda i, starts: (i, 0, 0)),
+                        pl.BlockSpec(memory_space=pltpu.SMEM),
+                    ],
+                    scratch_shapes=[pltpu.VMEM((N_DEV * WINDOW, d_model), BF16)],
+                ),
                 out_shape=[
                     jax.ShapeDtypeStruct((groups, seq, d_model), BF16),
-                    jax.ShapeDtypeStruct((8, 128), F32),
+                    jax.ShapeDtypeStruct((1, 1), F32),
                 ],
                 compiler_params=pltpu.CompilerParams(dimension_semantics=("arbitrary",), vmem_limit_bytes=VMEM_LIMIT),
-            )(back, back_pack, hidden_p, meta_p, msg)
+            )(starts, back, back_pack, hidden_p, meta_p, msg)
 
         def full_path():
             recv = pl.pallas_call(
@@ -754,11 +773,11 @@
                 ],
                 out_specs=[
                     pl.BlockSpec((2, seq, d_model), lambda i: (i, 0, 0)),
-                    pl.BlockSpec((8, 128), lambda i: (0, 0)),
+                    pl.BlockSpec(memory_space=pltpu.SMEM),
                 ],
                 out_shape=[
                     jax.ShapeDtypeStruct((groups, seq, d_model), BF16),
-                    jax.ShapeDtypeStruct((8, 128), F32),
+                    jax.ShapeDtypeStruct((1, 1), F32),
                 ],
                 compiler_params=pltpu.CompilerParams(dimension_semantics=("arbitrary",), vmem_limit_bytes=VMEM_LIMIT),
             )(ret, hidden_p, meta_p, msg)
@@ -766,7 +785,7 @@
         shared = jnp.sum(msg[:, 10, :].reshape(N_DEV // TEAM, TEAM, experts), axis=1)
         spilled = (jnp.max(msg[:, 9, 0]) > 0.0) | (jnp.max(shared) > POOL)
         out, aux = lax.cond(spilled, full_path, packed_path)
-        return out, aux[0, 0]
+        return out, aux.reshape(())
 
     by_group = P("ep")
     replicated = P()

time: 285 us -> 275 us (0.965)
  Pallas kernels: 281 us -> 272 us
    pallas_call x1, Pallas kernels: 134 us -> 102 us  [local_step(): pl.pallas_call(functools.partial(packed_front_kernel, heads=heads, head_d...]
    pallas_call x1, Pallas kernels: 122 us -> 147 us  [packed_path(): pl.pallas_call(packed_expert_kernel, name='packed_experts', grid=(2 * e_l...]
where the time goes in v1:
time: 275 us
  Pallas kernels  272 us (99%)
    pallas_call x1, Pallas kernels, packed_path(): pl.pallas_call(packed_expert_kernel, name='packed_experts', grid=(2 * e_l...  147 us
    pallas_call x1, Pallas kernels, local_step(): pl.pallas_call(functools.partial(packed_front_kernel, heads=heads, head_d...  102 us
    pallas_call x1, Pallas kernels, packed_path(): pl.pallas_call(functools.partial(packed_back_kernel, n_groups=groups * N_...  22.8 us

profile of v1, /device:TPU:1, one launch (start us, length us, event | category | flops | bytes accessed | tf_op | source)
XLA Modules:
  0.0 275.3 jit_solution(4930046795851356172)
XLA Ops:
  0.6 0.0 copy-start
  0.6 101.9 %packed_front.1 = (bf16[16,256,768]{2,1,0:T(8,128)(2,1)}, f32[16,8,256]{2,1,0:T(8,128)S(1)}, bf16[16,112,768]{2,1,0:T(8,128)(2,1)}, s32[8,128]{1,0:T(8,128)S(1)}...) custom-call(bf16[16,256,768]{2,1,0:T(8,128)(2,1)} %tokens_ref.1, s32[16,256]{1,0:T(8,128)} %pad_ref.1, ...), custom_call_target="tpu_custom_call" | custom-call | tf_op jit(solution)/shard_map/packed_front/pallas_call | solution.py:633
  102.5 0.6 slice_reduce_fusion
  103.8 0.6 reduce_max.19
  105.1 0.0 copy-done
  105.1 170.0 %conditional.1 = (bf16[16,256,768]{2,1,0:T(8,128)(2,1)}, f32[]{:T(128)}) conditional(s32[]{:T(128)} %convert_element_type.3, (bf16[8,512,768]{2,1,0:T(8,128)(2,1)}, bf16[16,112,768]{2,1,0:T(8,128)(2,1)}, f32[16,16,128]{2,1,0:T(8,128)S(1)}, bf16[8,768,3072]{2,1,0:T(8,128)(2,1)}, bf16[8,3072,768]{2,1,0:T(8,128)(2,1)}, ...), branch_computations={%region_3.0_spmd, %region_4.0_spmd} | conditional | bytes 16 | solution.py:787
  105.1 147.0 %packed_experts.1 = (bf16[128,32,768]{2,1,0:T(8,128)(2,1)}, bf16[16,112,768]{2,1,0:T(8,128)(2,1)}) custom-call(bf16[8,512,768]{2,1,0:T(8,128)(2,1)} %get-tuple-element.34.fix_ref, bf16[16,112,768]{2,1,0:T(8,128)(2,1)} %get-tuple-element.35.mine_ref, f32[16,16,128]{2,1,0:T(8,128)S(1)} %get-tuple-element.36.msg_ref, ...), custom_call_target="tpu_custom_call" | custom-call | tf_op jit(solution)/shard_map/cond/branch_0_fun/packed_experts/pallas_call | solution.py:678
  252.1 22.8 %packed_back.1 = (bf16[16,256,768]{2,1,0:T(8,128)(2,1)}, f32[1,1]{1,0:T(1,128)}) custom-call(s32[8,128]{1,0:T(8,128)S(1)} %get-tuple-element.33.starts_ref, bf16[128,32,768]{2,1,0:T(8,128)(2,1)} %get-tuple-element.39.fix_ref, bf16[16,112,768]{2,1,0:T(8,128)(2,1)} %get-tuple-element.40.pack_ref, bf16[16,256,768]{2,1,0:T(8,128)(2,1)} %get-tuple-element.41.hidden_ref, ...), custom_call_target="tpu_custom_call" | custom-call | tf_op jit(solution)/shard_map/cond/branch_0_fun/packed_back/pallas_call | solution.py:706
  (2 shorter events, 0.0 us)
Async XLA Ops:
  0.6 104.5 %copy-start = (f32[768]{0:T(1024)S(1)}, f32[768]{0:T(1024)}, u32[]{:S(2)}) copy-start(f32[768]{0:T(1024)} %norm_moe_ref.1) | copy-start | bytes 9220

commit v2 on v1

--- a/solution.py
+++ b/solution.py
@@ -260,7 +260,7 @@
 
 FIX = 8
 LOCAL = 48
-PACK = 112
+PACK = 104
 EXTRA = 32
 TEAM = 4
 POOL = 80
@@ -338,7 +338,7 @@
     meta_row = lax.broadcasted_iota(jnp.int32, (8, seq), 0)
 
     def window_start():
-        return jnp.minimum(jnp.floor(count_s[3] * (1.0 / 16)) * 16.0, float(PACK - WINDOW))
+        return jnp.minimum(jnp.floor(count_s[3] * (1.0 / 8)) * 8.0, float(PACK - WINDOW))
 
     for grp in range(2):
         p = gate_probs[:, grp * seq:(grp + 1) * seq]
@@ -473,8 +473,23 @@
         settle(msg_ref.at[others], msg_recv)
 
 
+def gate_rows(meta, count, base):
+    cols = meta.T
+    ids = lax.broadcasted_iota(jnp.int32, (cols.shape[0], count), 1) + base
+    first = ids == cols[:, 0:1].astype(jnp.int32)
+    second = ids == cols[:, 1:2].astype(jnp.int32)
+    return jnp.where(first, cols[:, 2:3], jnp.where(second, cols[:, 3:4], 0.0)).astype(BF16)
+
+
+def combine_fixed(fix_ref, hidden_ref, meta_ref, part_ref):
+    experts, rows, d_model = fix_ref.shape
+    z = fix_ref[...].reshape(experts * rows, d_model)
+    for grp in range(2):
+        part_ref[grp] = hidden_ref[grp].astype(F32) + dot(gate_rows(meta_ref[grp], experts * rows, 0), z)
+
+
 def packed_expert_kernel(
-    fix_ref, mine_ref, msg_ref, w_in_ref, w_out_ref, back_ref, back_pack_ref,
+    fix_ref, mine_ref, msg_ref, w_in_ref, w_out_ref, hidden_ref, meta_ref, back_ref, back_pack_ref, part_ref,
     act_s, x_s, z_s, zx_s, code_s, pack_ref, pack_s, in_send, in_recv, fix_send, fix_recv, pack_send, pack_recv, own_sem,
 ):
     step = pl.program_id(0)
@@ -559,43 +574,42 @@
                 remote(pack_s.at[place - 1], back_pack_ref.at[me], pack_send, pack_recv, ORDER[place - 1], 2)
         remote(pack_s.at[N_DEV - 1], back_pack_ref.at[me], pack_send, pack_recv, ORDER[N_DEV - 1], 2)
         settle(z_s.at[:, pl.ds(0, per_src), :], own_sem.at[1])
+        settle(back_ref.at[pl.ds(0, (N_DEV - 1) * n_exp)], fix_recv)
+        groups, seq, _ = hidden_ref.shape
+        experts = back_ref.shape[0]
+        pltpu.emit_pipeline(
+            combine_fixed,
+            grid=(groups // 2,),
+            in_specs=[
+                pl.BlockSpec((experts, FIX, d_model), lambda i: (0, i // 2, 0)),
+                pl.BlockSpec((2, seq, d_model), lambda i: (i, 0, 0)),
+                pl.BlockSpec((2, 8, seq), lambda i: (i, 0, 0)),
+            ],
+            out_specs=[pl.BlockSpec((2, seq, d_model), lambda i: (i, 0, 0))],
+        )(back_ref, hidden_ref, meta_ref, part_ref)
         settle(pack_s.at[0], own_sem.at[2])
         settle(mine_ref.at[others], in_send)
         settle(z_s.at[:, pl.ds(0, (N_DEV - 1) * per_src), :], fix_send)
         settle(pack_s.at[others], pack_send)
-        settle(back_ref.at[pl.ds(0, (N_DEV - 1) * n_exp)], fix_recv)
         settle(back_pack_ref.at[others], pack_recv)
 
 
-def packed_back_kernel(starts_ref, fix_ref, pack_ref, hidden_ref, meta_ref, msg_ref, out_ref, aux_ref, window_s, *, n_groups):
-    experts, rows, d_model = fix_ref.shape
-    seq = hidden_ref.shape[1]
-    z = fix_ref[...].reshape(experts * rows, d_model)
+def packed_back_kernel(starts_ref, pack_ref, part_ref, meta_ref, msg_ref, out_ref, aux_ref, window_s, *, n_groups, experts):
+    seq = part_ref.shape[1]
+    e_loc = experts // N_DEV
     step = pl.program_id(0)
 
     @pl.when(lax.rem(step, 2) == 0)
     def _():
         for dev in range(N_DEV):
-            start = pl.multiple_of(starts_ref[step // 2, dev * (experts // N_DEV)], 16)
+            start = pl.multiple_of(starts_ref[step // 2, dev * e_loc], 8)
             window_s[dev * WINDOW:(dev + 1) * WINDOW, :] = pack_ref[dev, pl.ds(start, WINDOW), :]
 
-    zx = window_s[...]
-    fix_id = lax.broadcasted_iota(jnp.int32, (seq, experts * rows), 1)
-    pack_id = lax.broadcasted_iota(jnp.int32, (seq, N_DEV * WINDOW), 1) + experts * rows
     for grp in range(2):
-        meta = meta_ref[grp].T
-        c1 = meta[:, 0:1].astype(jnp.int32)
-        c2 = meta[:, 1:2].astype(jnp.int32)
-        g1 = meta[:, 2:3]
-        g2 = meta[:, 3:4]
-
-        def gates(ids):
-            return jnp.where(ids == c1, g1, jnp.where(ids == c2, g2, 0.0)).astype(BF16)
-
-        moe = dot(gates(fix_id), z) + dot(gates(pack_id), zx)
-        out_ref[grp] = (hidden_ref[grp].astype(F32) + moe).astype(BF16)
-
-    @pl.when(pl.program_id(0) == 0)
+        moe = dot(gate_rows(meta_ref[grp], N_DEV * WINDOW, experts * FIX), window_s[...])
+        out_ref[grp] = (part_ref[grp] + moe).astype(BF16)
+
+    @pl.when(step == 0)
     def _():
         aux_ref[0, 0] = jnp.sum(msg_ref[:, 0:8, :]) * (experts / n_groups)
 
@@ -675,7 +689,7 @@
         )(tokens, pad_mask, second_draw, choices.transpose(0, 2, 1), norm_attn, wq, wk, wv, wo, norm_moe, w_gate)
 
         def packed_path():
-            back, back_pack = pl.pallas_call(
+            back, back_pack, part = pl.pallas_call(
                 packed_expert_kernel,
                 name="packed_experts",
                 grid=(2 * e_loc,),
@@ -684,11 +698,13 @@
                     whole((N_DEV, PACK, d_model)), whole((N_DEV, 16, 128)),
                     pl.BlockSpec((1, d_model, ff), lambda i: (lax.rem(i, e_loc), 0, 0)),
                     pl.BlockSpec((1, ff, d_model), lambda i: (lax.rem(i, e_loc), 0, 0)),
+                    anywhere, anywhere,
                 ],
-                out_specs=[anywhere, anywhere],
+                out_specs=[anywhere, anywhere, anywhere],
                 out_shape=[
                     jax.ShapeDtypeStruct((experts, fix_rows, d_model), BF16),
                     jax.ShapeDtypeStruct((N_DEV, PACK, d_model), BF16),
+                    jax.ShapeDtypeStruct((groups, seq, d_model), F32),
                 ],
                 scratch_shapes=[
                     pltpu.VMEM((N_DEV * fix_rows, ff), BF16),
@@ -702,15 +718,14 @@
                 ],
                 compiler_params=pltpu.CompilerParams(
                     dimension_semantics=("arbitrary",), collective_id=1, has_side_effects=True, vmem_limit_bytes=VMEM_LIMIT),
-            )(fix, mine, msg, w_in, w_out)
+            )(fix, mine, msg, w_in, w_out, hidden_p, meta_p)
             return pl.pallas_call(
-                functools.partial(packed_back_kernel, n_groups=groups * N_DEV),
+                functools.partial(packed_back_kernel, n_groups=groups * N_DEV, experts=experts),
                 name="packed_back",
                 grid_spec=pltpu.PrefetchScalarGridSpec(
                     num_scalar_prefetch=1,
                     grid=(steps,),
                     in_specs=[
-                        pl.BlockSpec((experts, FIX, d_model), lambda i, starts: (0, i // 2, 0)),
                         pl.BlockSpec((N_DEV, PACK, d_model), lambda i, starts: (0, 0, 0), pipeline_mode=pl.Buffered(1)),
                         pl.BlockSpec((2, seq, d_model), lambda i, starts: (i, 0, 0)),
                         pl.BlockSpec((2, 8, seq), lambda i, starts: (i, 0, 0)),
@@ -727,7 +742,7 @@
                     jax.ShapeDtypeStruct((1, 1), F32),
                 ],
                 compiler_params=pltpu.CompilerParams(dimension_semantics=("arbitrary",), vmem_limit_bytes=VMEM_LIMIT),
-            )(starts, back, back_pack, hidden_p, meta_p, msg)
+            )(starts, back_pack, part, meta_p, msg)
 
         def full_path():
             recv = pl.pallas_call(

time: 275 us -> 264 us (0.960)
  Pallas kernels: 272 us -> 260 us
    pallas_call x1, Pallas kernels: 22.8 us -> 16 us  [packed_path(): pl.pallas_call(functools.partial(packed_back_kernel, n_groups=groups * N_...]
    pallas_call x1, Pallas kernels: 147 us -> 142 us  [packed_path(): pl.pallas_call(packed_expert_kernel, name='packed_experts', grid=(2 * e_l...]
where the time goes in v2:
time: 264 us; the launch traced here: 263 us
  Pallas kernels  260 us (98%)
    pallas_call x1, Pallas kernels, packed_path(): pl.pallas_call(packed_expert_kernel, name='packed_experts', grid=(2 * e_l...  142 us
    pallas_call x1, Pallas kernels, local_step(): pl.pallas_call(functools.partial(packed_front_kernel, heads=heads, head_d...  102 us
    pallas_call x1, Pallas kernels, packed_path(): pl.pallas_call(functools.partial(packed_back_kernel, n_groups=groups * N_...  16 us

profile of v2, /device:TPU:1, one launch (start us, length us, event | category | flops | bytes accessed | tf_op | source)
XLA Modules:
  0.0 263.4 jit_solution(1252020124018453870)
XLA Ops:
  0.6 0.0 copy-start
  0.6 101.8 %packed_front.1 = (bf16[16,256,768]{2,1,0:T(8,128)(2,1)}, f32[16,8,256]{2,1,0:T(8,128)S(1)}, bf16[16,104,768]{2,1,0:T(8,128)(2,1)}, s32[8,128]{1,0:T(8,128)S(1)}...) custom-call(bf16[16,256,768]{2,1,0:T(8,128)(2,1)} %tokens_ref.1, s32[16,256]{1,0:T(8,128)} %pad_ref.1, ...), custom_call_target="tpu_custom_call" | custom-call | tf_op jit(solution)/shard_map/packed_front/pallas_call | solution.py:647
  102.5 0.6 slice_reduce_fusion
  103.8 0.6 reduce_max.19
  105.0 0.0 copy-done
  105.1 158.2 %conditional.1 = (bf16[16,256,768]{2,1,0:T(8,128)(2,1)}, f32[]{:T(128)}) conditional(s32[]{:T(128)} %convert_element_type.3, (bf16[8,512,768]{2,1,0:T(8,128)(2,1)}, bf16[16,104,768]{2,1,0:T(8,128)(2,1)}, f32[16,16,128]{2,1,0:T(8,128)S(1)}, bf16[8,768,3072]{2,1,0:T(8,128)(2,1)}, bf16[8,3072,768]{2,1,0:T(8,128)(2,1)}, ...), branch_computations={%region_3.0_spmd, %region_4.0_spmd} | conditional | bytes 16 | solution.py:802
  105.1 142.0 %packed_experts.1 = (bf16[128,32,768]{2,1,0:T(8,128)(2,1)}, bf16[16,104,768]{2,1,0:T(8,128)(2,1)}, f32[16,256,768]{2,1,0:T(8,128)}) custom-call(bf16[8,512,768]{2,1,0:T(8,128)(2,1)} %get-tuple-element.34.fix_ref, bf16[16,104,768]{2,1,0:T(8,128)(2,1)} %get-tuple-element.35.mine_ref, f32[16,16,128]{2,1,0:T(8,128)S(1)} %get-tuple-element.36.msg_ref, ...), custom_call_target="tpu_custom_call" | custom-call | tf_op jit(solution)/shard_map/cond/branch_0_fun/packed_experts/pallas_call | solution.py:692
  247.1 16.0 %packed_back.1 = (bf16[16,256,768]{2,1,0:T(8,128)(2,1)}, f32[1,1]{1,0:T(1,128)}) custom-call(s32[8,128]{1,0:T(8,128)S(1)} %get-tuple-element.33.starts_ref, bf16[16,104,768]{2,1,0:T(8,128)(2,1)} %get-tuple-element.41.pack_ref, f32[16,256,768]{2,1,0:T(8,128)} %get-tuple-element.42.part_ref, f32[16,8,256]{2,1,0:T(8,128)S(1)} %get-tuple-element.40.meta_ref, ...), custom_call_target="tpu_custom_call" | custom-call | tf_op jit(solution)/shard_map/cond/branch_0_fun/packed_back/pallas_call | solution.py:722
  (2 shorter events, 0.0 us)
Async XLA Ops:
  0.6 104.4 %copy-start = (f32[768]{0:T(1024)S(1)}, f32[768]{0:T(1024)}, u32[]{:S(2)}) copy-start(f32[768]{0:T(1024)} %norm_moe_ref.1) | copy-start | bytes 9220

commit v3 on v2

--- a/solution.py
+++ b/solution.py
@@ -446,11 +446,11 @@
         over = jnp.where((count_s[1] > PACK) | (count_s[2] > EXTRA), 1.0, 0.0)
         over = jnp.max(jnp.max(over.reshape(N_DEV, e_loc, 128), axis=1), axis=0, keepdims=True)
         over = jnp.maximum(over, jnp.max(flag_s[...], axis=0, keepdims=True))
-        tally = count_s[2].T[0:1, :]
+        tally = count_s[2].T[0:1, :] + over * 1024.0
         for dev in range(N_DEV):
             msg_s[dev, 0:8] = aux_s[...]
             lower = lax.broadcasted_iota(jnp.int32, (8, 128), 0)
-            msg_s[dev, 8:16] = jnp.where(lower == 0, code_s[dev:dev + 1, :], jnp.where(lower == 1, over, jnp.where(lower == 2, tally, 0.0)))
+            msg_s[dev, 8:16] = jnp.where(lower == 0, code_s[dev:dev + 1, :], jnp.where(lower == 1, tally, 0.0))
         for place, mask in enumerate(ORDER):
             dev = partner(me, mask)
             remote(msg_s.at[dev], msg_ref.at[place], msg_send, msg_recv, dev, mask, 1)
@@ -490,7 +490,7 @@
 
 def packed_expert_kernel(
     fix_ref, mine_ref, msg_ref, w_in_ref, w_out_ref, hidden_ref, meta_ref, back_ref, back_pack_ref, part_ref,
-    act_s, x_s, z_s, zx_s, code_s, pack_ref, pack_s, in_send, in_recv, fix_send, fix_recv, pack_send, pack_recv, own_sem,
+    w1_s, w2_s, w_sem, act_s, x_s, z_s, zx_s, code_s, pack_ref, pack_s, in_send, in_recv, fix_send, fix_recv, pack_send, pack_recv, own_sem,
 ):
     step = pl.program_id(0)
     n_exp = pl.num_programs(0) // 2
@@ -499,14 +499,15 @@
     rows = fix_ref.shape[1]
     d_model = fix_ref.shape[2]
     ff = w_in_ref.shape[2]
+    slot = lax.rem(step, 2)
     per_src = rows // N_DEV
     chunk = 1024
 
     def mlp(x):
         for f in range(ff // chunk):
-            act = dot(x, w_in_ref[0, :, pl.ds(f * chunk, chunk)])
+            act = dot(x, w1_s[slot, :, pl.ds(f * chunk, chunk)])
             act_s[0:x.shape[0], pl.ds(f * chunk, chunk)] = jnp.maximum(act, 0.0).astype(BF16)
-        return dot(act_s[0:x.shape[0], :], w_out_ref[0]).astype(BF16)
+        return dot(act_s[0:x.shape[0], :], w2_s[slot]).astype(BF16)
 
     def spread(place):
         ids = lax.broadcasted_iota(jnp.int32, (x_s.shape[0] * POOL, PACK), 0).astype(F32) + 1.0
@@ -525,12 +526,28 @@
 
     others = pl.ds(0, N_DEV - 1)
 
+    def weights(which, at):
+        return (
+            pltpu.make_async_copy(w_in_ref.at[which], w1_s.at[at], w_sem.at[0, at]),
+            pltpu.make_async_copy(w_out_ref.at[which], w2_s.at[at], w_sem.at[1, at]),
+        )
+
     @pl.when(step == 0)
     def _():
+        for copy in weights(e, slot):
+            copy.start()
         greet(me)
         pl.semaphore_wait(pltpu.get_barrier_semaphore(), N_DEV - 1)
         for place, mask in enumerate(ORDER):
             remote(mine_ref.at[partner(me, mask)], pack_ref.at[place], in_send, in_recv, mask, 0)
+
+    @pl.when(step < 2 * n_exp - 1)
+    def _():
+        for copy in weights(lax.rem(step + 1, n_exp), 1 - slot):
+            copy.start()
+
+    for copy in weights(e, slot):
+        copy.wait()
 
     @pl.when(step < n_exp)
     def _():
@@ -595,19 +612,18 @@
 
 
 def packed_back_kernel(starts_ref, pack_ref, part_ref, meta_ref, msg_ref, out_ref, aux_ref, window_s, *, n_groups, experts):
-    seq = part_ref.shape[1]
+    groups, seq, _ = part_ref.shape
     e_loc = experts // N_DEV
     step = pl.program_id(0)
-
-    @pl.when(lax.rem(step, 2) == 0)
-    def _():
-        for dev in range(N_DEV):
-            start = pl.multiple_of(starts_ref[step // 2, dev * e_loc], 8)
-            window_s[dev * WINDOW:(dev + 1) * WINDOW, :] = pack_ref[dev, pl.ds(start, WINDOW), :]
-
-    for grp in range(2):
-        moe = dot(gate_rows(meta_ref[grp], N_DEV * WINDOW, experts * FIX), window_s[...])
-        out_ref[grp] = (part_ref[grp] + moe).astype(BF16)
+    for dev in range(N_DEV):
+        start = pl.multiple_of(starts_ref[step, dev * e_loc], 8)
+        window_s[dev * WINDOW:(dev + 1) * WINDOW, :] = pack_ref[dev, pl.ds(start, WINDOW), :]
+
+    for grp in range(0, groups, 2):
+        gates = jnp.concatenate([gate_rows(meta_ref[grp + i], N_DEV * WINDOW, experts * FIX) for i in range(2)], axis=0)
+        moe = dot(gates, window_s[...])
+        for i in range(2):
+            out_ref[grp + i] = (part_ref[grp + i] + moe[i * seq:(i + 1) * seq]).astype(BF16)
 
     @pl.when(step == 0)
     def _():
@@ -669,8 +685,8 @@
                 pltpu.VMEM((2 * seq, hw), BF16),
                 pltpu.VMEM((hw, 2 * seq), BF16),
                 pltpu.VMEM((hw, 2 * seq), BF16),
-                pltpu.VMEM((2, 4, seq, seq), F32),
-                pltpu.VMEM((2, 4, seq, seq), BF16),
+                pltpu.VMEM((2, heads, seq, seq), F32),
+                pltpu.VMEM((2, heads, seq, seq), BF16),
                 pltpu.VMEM((3 * experts, d_model), BF16),
                 pltpu.VMEM((4 * seq, d_model), BF16),
                 pltpu.VMEM((8, 4 * seq), jnp.int32),
@@ -696,9 +712,7 @@
                 in_specs=[
                     pl.BlockSpec((1, N_DEV * fix_rows, d_model), lambda i: (jnp.minimum(i, e_loc - 1), 0, 0)),
                     whole((N_DEV, PACK, d_model)), whole((N_DEV, 16, 128)),
-                    pl.BlockSpec((1, d_model, ff), lambda i: (lax.rem(i, e_loc), 0, 0)),
-                    pl.BlockSpec((1, ff, d_model), lambda i: (lax.rem(i, e_loc), 0, 0)),
-                    anywhere, anywhere,
+                    anywhere, anywhere, anywhere, anywhere,
                 ],
                 out_specs=[anywhere, anywhere, anywhere],
                 out_shape=[
@@ -707,6 +721,9 @@
                     jax.ShapeDtypeStruct((groups, seq, d_model), F32),
                 ],
                 scratch_shapes=[
+                    pltpu.VMEM((2, d_model, ff), BF16),
+                    pltpu.VMEM((2, ff, d_model), BF16),
+                    dma((2, 2)),
                     pltpu.VMEM((N_DEV * fix_rows, ff), BF16),
                     pltpu.VMEM((e_loc, N_DEV // TEAM * POOL, d_model), BF16),
                     pltpu.VMEM((e_loc, N_DEV * fix_rows, d_model), BF16),
@@ -724,15 +741,15 @@
                 name="packed_back",
                 grid_spec=pltpu.PrefetchScalarGridSpec(
                     num_scalar_prefetch=1,
-                    grid=(steps,),
+                    grid=(quads,),
                     in_specs=[
                         pl.BlockSpec((N_DEV, PACK, d_model), lambda i, starts: (0, 0, 0), pipeline_mode=pl.Buffered(1)),
-                        pl.BlockSpec((2, seq, d_model), lambda i, starts: (i, 0, 0)),
-                        pl.BlockSpec((2, 8, seq), lambda i, starts: (i, 0, 0)),
+                        pl.BlockSpec((4, seq, d_model), lambda i, starts: (i, 0, 0)),
+                        pl.BlockSpec((4, 8, seq), lambda i, starts: (i, 0, 0)),
                         pl.BlockSpec((N_DEV, 16, 128), lambda i, starts: (0, 0, 0), pipeline_mode=pl.Buffered(1)),
                     ],
                     out_specs=[
-                        pl.BlockSpec((2, seq, d_model), lambda i, starts: (i, 0, 0)),
+                        pl.BlockSpec((4, seq, d_model), lambda i, starts: (i, 0, 0)),
                         pl.BlockSpec(memory_space=pltpu.SMEM),
                     ],
                     scratch_shapes=[pltpu.VMEM((N_DEV * WINDOW, d_model), BF16)],
@@ -797,8 +814,8 @@
                 compiler_params=pltpu.CompilerParams(dimension_semantics=("arbitrary",), vmem_limit_bytes=VMEM_LIMIT),
             )(ret, hidden_p, meta_p, msg)
 
-        shared = jnp.sum(msg[:, 10, :].reshape(N_DEV // TEAM, TEAM, experts), axis=1)
-        spilled = (jnp.max(msg[:, 9, 0]) > 0.0) | (jnp.max(shared) > POOL)
+        shared = jnp.sum(msg[:, 9, :].reshape(N_DEV // TEAM, TEAM, experts), axis=1)
+        spilled = jnp.max(shared) > POOL
         out, aux = lax.cond(spilled, full_path, packed_path)
         return out, aux.reshape(())
 

time: 264 us -> 255 us (0.966)
  Pallas kernels: 260 us -> 252 us
    pallas_call x1, Pallas kernels: 142 us -> 138 us  [packed_path(): pl.pallas_call(packed_expert_kernel, name='packed_experts', grid=(2 * e_l...]
where the time goes in v3:
time: 255 us; the launch traced here: 254 us
  Pallas kernels  252 us (99%)
    pallas_call x1, Pallas kernels, packed_path(): pl.pallas_call(packed_expert_kernel, name='packed_experts', grid=(2 * e_l...  138 us
    pallas_call x1, Pallas kernels, local_step(): pl.pallas_call(functools.partial(packed_front_kernel, heads=heads, head_d...  99.6 us
    pallas_call x1, Pallas kernels, packed_path(): pl.pallas_call(functools.partial(packed_back_kernel, n_groups=groups * N_...  14 us

profile of v3, /device:TPU:1, one launch (start us, length us, event | category | flops | bytes accessed | tf_op | source)
XLA Modules:
  0.0 254.3 jit_solution(14240018255773940106)
XLA Ops:
  0.6 0.0 copy-start
  0.6 99.6 %packed_front.1 = (bf16[16,256,768]{2,1,0:T(8,128)(2,1)}, f32[16,8,256]{2,1,0:T(8,128)S(1)}, bf16[16,104,768]{2,1,0:T(8,128)(2,1)}, s32[8,128]{1,0:T(8,128)S(1)}...) custom-call(bf16[16,256,768]{2,1,0:T(8,128)(2,1)} %tokens_ref.1, s32[16,256]{1,0:T(8,128)} %pad_ref.1, ...), custom_call_target="tpu_custom_call" | custom-call | tf_op jit(solution)/shard_map/packed_front/pallas_call | solution.py:663
  100.3 0.6 reduce_max.9
  101.6 0.0 copy-done
  101.6 152.5 %conditional.1 = (bf16[16,256,768]{2,1,0:T(8,128)(2,1)}, f32[]{:T(128)}) conditional(s32[]{:T(128)} %convert_element_type.3, (bf16[8,512,768]{2,1,0:T(8,128)(2,1)}, bf16[16,104,768]{2,1,0:T(8,128)(2,1)}, f32[16,16,128]{2,1,0:T(8,128)S(1)}, bf16[8,768,3072]{2,1,0:T(8,128)(2,1)}, bf16[8,3072,768]{2,1,0:T(8,128)(2,1)}, ...), branch_computations={%region_2.0_spmd, %region_3.0_spmd} | conditional | bytes 16 | solution.py:819
  101.6 138.3 %packed_experts.1 = (bf16[128,32,768]{2,1,0:T(8,128)(2,1)}, bf16[16,104,768]{2,1,0:T(8,128)(2,1)}, f32[16,256,768]{2,1,0:T(8,128)}) custom-call(bf16[8,512,768]{2,1,0:T(8,128)(2,1)} %get-tuple-element.34.fix_ref, bf16[16,104,768]{2,1,0:T(8,128)(2,1)} %get-tuple-element.35.mine_ref, f32[16,16,128]{2,1,0:T(8,128)S(1)} %get-tuple-element.36.msg_ref, ...), custom_call_target="tpu_custom_call" | custom-call | tf_op jit(solution)/shard_map/cond/branch_0_fun/packed_experts/pallas_call | solution.py:708
  239.9 14.0 %packed_back.1 = (bf16[16,256,768]{2,1,0:T(8,128)(2,1)}, f32[1,1]{1,0:T(1,128)}) custom-call(s32[8,128]{1,0:T(8,128)S(1)} %get-tuple-element.33.starts_ref, bf16[16,104,768]{2,1,0:T(8,128)(2,1)} %get-tuple-element.41.pack_ref, f32[16,256,768]{2,1,0:T(8,128)} %get-tuple-element.42.part_ref, f32[16,8,256]{2,1,0:T(8,128)S(1)} %get-tuple-element.40.meta_ref, ...), custom_call_target="tpu_custom_call" | custom-call | tf_op jit(solution)/shard_map/cond/branch_0_fun/packed_back/pallas_call | solution.py:739
  (2 shorter events, 0.0 us)
Async XLA Ops:
  0.6 100.9 %copy-start = (f32[768]{0:T(1024)S(1)}, f32[768]{0:T(1024)}, u32[]{:S(2)}) copy-start(f32[768]{0:T(1024)} %norm_moe_ref.1) | copy-start | bytes 9220

commit v4 on v3

--- a/solution.py
+++ b/solution.py
@@ -12,6 +12,7 @@
 F32 = jnp.float32
 BF16 = jnp.bfloat16
 ORDER = (0, 9, 2, 11, 4, 13, 6, 15, 8, 1, 10, 3, 12, 5, 14, 7)
+SENDS = tuple((ORDER.index(mask), mask) for mask in (6, 8, 10, 4, 12, 2, 14, 1, 7, 9, 11, 5, 13, 3, 15, 0))
 VMEM_LIMIT = 62 * 1024 * 1024
 
 
@@ -123,7 +124,7 @@
     per_src = steps * rows
 
     def send_pair(pair):
-        for place, mask in enumerate(ORDER):
+        for place, mask in SENDS:
             dev = partner(me, mask)
             src = send_s.at[pair, dev]
             dst = recv_ref.at[:, pl.ds(pl.multiple_of(place * per_src + pair * rows, rows), rows), :]
@@ -210,7 +211,7 @@
     def _():
         pl.semaphore_wait(pltpu.get_barrier_semaphore(), N_DEV - 1)
 
-    for place, mask in enumerate(ORDER):
+    for place, mask in SENDS:
         dev = partner(me, mask)
         src = z_s.at[e, pl.ds(place * per_src, per_src), :]
         dst = ret_ref.at[me * n_exp + e]
@@ -297,7 +298,7 @@
                 device_id=(dev,), device_id_type=MESH).start()
 
     def send_quad(which):
-        for place, mask in enumerate(ORDER):
+        for place, mask in SENDS:
             dev = partner(me, mask)
             row = pl.multiple_of(place * quads * FIX + which * FIX, FIX)
             remote(fix_s.at[which, dev], fix_ref.at[:, pl.ds(row, FIX), :], fix_send, fix_recv, dev, mask, 0)
@@ -420,12 +421,12 @@
             return dot(jnp.where(hit, 1.0, 0.0).astype(BF16), b_s[skip:, :]).astype(BF16)
 
         per_dev = e_loc * FIX
-        for base in range(0, N_DEV, 4):
-            rows = gather(0, base * per_dev, 4 * per_dev, 0)
-            fix_s[quad, base:base + 4] = rows.reshape(4, e_loc, FIX, d_model)
-        for base in range(0, N_DEV, 4):
-            rows = gather(2, base * LOCAL, 4 * LOCAL, 2 * seq)
-            local_s[base:base + 4, pl.ds(pl.multiple_of(quad * LOCAL, LOCAL), LOCAL), :] = rows.reshape(4, LOCAL, d_model)
+        for base in range(0, N_DEV, 8):
+            rows = gather(0, base * per_dev, 8 * per_dev, 0)
+            fix_s[quad, base:base + 8] = rows.reshape(8, e_loc, FIX, d_model)
+        for base in range(0, N_DEV, 8):
+            rows = gather(2, base * LOCAL, 8 * LOCAL, 2 * seq)
+            local_s[base:base + 8, pl.ds(pl.multiple_of(quad * LOCAL, LOCAL), LOCAL), :] = rows.reshape(8, LOCAL, d_model)
 
         def per_device(value):
             return value.reshape(N_DEV, e_loc, 128)[:, 0, :]
@@ -451,7 +452,7 @@
             msg_s[dev, 0:8] = aux_s[...]
             lower = lax.broadcasted_iota(jnp.int32, (8, 128), 0)
             msg_s[dev, 8:16] = jnp.where(lower == 0, code_s[dev:dev + 1, :], jnp.where(lower == 1, tally, 0.0))
-        for place, mask in enumerate(ORDER):
+        for place, mask in SENDS:
             dev = partner(me, mask)
             remote(msg_s.at[dev], msg_ref.at[place], msg_send, msg_recv, dev, mask, 1)
 
@@ -538,7 +539,7 @@
             copy.start()
         greet(me)
         pl.semaphore_wait(pltpu.get_barrier_semaphore(), N_DEV - 1)
-        for place, mask in enumerate(ORDER):
+        for place, mask in SENDS:
             remote(mine_ref.at[partner(me, mask)], pack_ref.at[place], in_send, in_recv, mask, 0)
 
     @pl.when(step < 2 * n_exp - 1)
@@ -552,7 +553,7 @@
     @pl.when(step < n_exp)
     def _():
         z_s[e] = mlp(fix_ref[0])
-        for place, mask in enumerate(ORDER):
+        for place, mask in SENDS:
             remote(z_s.at[e, pl.ds(place * per_src, per_src), :], back_ref.at[me * n_exp + e], fix_send, fix_recv, mask, 1)
 
     @pl.when(step == n_exp)
@@ -583,13 +584,16 @@
 
     @pl.when(step == 2 * n_exp - 1)
     def _():
-        for place, mask in enumerate(ORDER):
+        ready = None
+        for place, mask in SENDS:
             z = zx_s[:, pl.ds(place // TEAM * POOL, POOL), :].reshape(x_s.shape[0] * POOL, d_model)
             pack_s[place] = lax.dot_general(
                 spread(place), z, (((0,), (0,)), ((), ())), preferred_element_type=F32).astype(BF16)
-            if place > 0:
-                remote(pack_s.at[place - 1], back_pack_ref.at[me], pack_send, pack_recv, ORDER[place - 1], 2)
-        remote(pack_s.at[N_DEV - 1], back_pack_ref.at[me], pack_send, pack_recv, ORDER[N_DEV - 1], 2)
+            if ready is not None:
+                remote(pack_s.at[ready[0]], back_pack_ref.at[me], pack_send, pack_recv, ready[1], 2)
+            ready = (place, mask)
+        remote(pack_s.at[ready[0]], back_pack_ref.at[me], pack_send, pack_recv, ready[1], 2)
+
         settle(z_s.at[:, pl.ds(0, per_src), :], own_sem.at[1])
         settle(back_ref.at[pl.ds(0, (N_DEV - 1) * n_exp)], fix_recv)
         groups, seq, _ = hidden_ref.shape

time: 255 us -> 244 us (0.957)
  Pallas kernels: 252 us -> 241 us
    pallas_call x1, Pallas kernels: 138 us -> 131 us  [packed_path(): pl.pallas_call(packed_expert_kernel, name='packed_experts', grid=(2 * e_l...]
    pallas_call x1, Pallas kernels: 99.6 us -> 95.9 us  [local_step(): pl.pallas_call(functools.partial(packed_front_kernel, heads=heads, head_d...]
where the time goes in v4:
time: 244 us
  Pallas kernels  241 us (99%)
    pallas_call x1, Pallas kernels, packed_path(): pl.pallas_call(packed_expert_kernel, name='packed_experts', grid=(2 * e_l...  131 us
    pallas_call x1, Pallas kernels, local_step(): pl.pallas_call(functools.partial(packed_front_kernel, heads=heads, head_d...  95.9 us
    pallas_call x1, Pallas kernels, packed_path(): pl.pallas_call(functools.partial(packed_back_kernel, n_groups=groups * N_...  14 us

profile of v4, /device:TPU:1, one launch (start us, length us, event | category | flops | bytes accessed | tf_op | source)
XLA Modules:
  0.0 243.5 jit_solution(10848761994701558784)
XLA Ops:
  0.6 0.0 copy-start
  0.6 95.9 %packed_front.1 = (bf16[16,256,768]{2,1,0:T(8,128)(2,1)}, f32[16,8,256]{2,1,0:T(8,128)S(1)}, bf16[16,104,768]{2,1,0:T(8,128)(2,1)}, s32[8,128]{1,0:T(8,128)S(1)}...) custom-call(bf16[16,256,768]{2,1,0:T(8,128)(2,1)} %tokens_ref.1, s32[16,256]{1,0:T(8,128)} %pad_ref.1, ...), custom_call_target="tpu_custom_call" | custom-call | tf_op jit(solution)/shard_map/packed_front/pallas_call | solution.py:667
  96.6 0.6 reduce_max.9
  97.9 0.0 copy-done
  97.9 145.5 %conditional.1 = (bf16[16,256,768]{2,1,0:T(8,128)(2,1)}, f32[]{:T(128)}) conditional(s32[]{:T(128)} %convert_element_type.3, (bf16[8,512,768]{2,1,0:T(8,128)(2,1)}, bf16[16,104,768]{2,1,0:T(8,128)(2,1)}, f32[16,16,128]{2,1,0:T(8,128)S(1)}, bf16[8,768,3072]{2,1,0:T(8,128)(2,1)}, bf16[8,3072,768]{2,1,0:T(8,128)(2,1)}, ...), branch_computations={%region_2.0_spmd, %region_3.0_spmd} | conditional | bytes 16 | solution.py:823
  97.9 131.3 %packed_experts.1 = (bf16[128,32,768]{2,1,0:T(8,128)(2,1)}, bf16[16,104,768]{2,1,0:T(8,128)(2,1)}, f32[16,256,768]{2,1,0:T(8,128)}) custom-call(bf16[8,512,768]{2,1,0:T(8,128)(2,1)} %get-tuple-element.34.fix_ref, bf16[16,104,768]{2,1,0:T(8,128)(2,1)} %get-tuple-element.35.mine_ref, f32[16,16,128]{2,1,0:T(8,128)S(1)} %get-tuple-element.36.msg_ref, ...), custom_call_target="tpu_custom_call" | custom-call | tf_op jit(solution)/shard_map/cond/branch_0_fun/packed_experts/pallas_call | solution.py:712
  229.2 14.0 %packed_back.1 = (bf16[16,256,768]{2,1,0:T(8,128)(2,1)}, f32[1,1]{1,0:T(1,128)}) custom-call(s32[8,128]{1,0:T(8,128)S(1)} %get-tuple-element.33.starts_ref, bf16[16,104,768]{2,1,0:T(8,128)(2,1)} %get-tuple-element.41.pack_ref, f32[16,256,768]{2,1,0:T(8,128)} %get-tuple-element.42.part_ref, f32[16,8,256]{2,1,0:T(8,128)S(1)} %get-tuple-element.40.meta_ref, ...), custom_call_target="tpu_custom_call" | custom-call | tf_op jit(solution)/shard_map/cond/branch_0_fun/packed_back/pallas_call | solution.py:743
  (2 shorter events, 0.0 us)
Async XLA Ops:
  0.6 97.2 %copy-start = (f32[768]{0:T(1024)S(1)}, f32[768]{0:T(1024)}, u32[]{:S(2)}) copy-start(f32[768]{0:T(1024)} %norm_moe_ref.1) | copy-start | bytes 9220
